TPU v7x, 128 devices: a whole 4x4x4 slice. The times are simulated.
128 devices in a mesh: dp: 64 (over z, y, x), fsdp: 2 (over core).
Axes of the slice: x: 4, y: 4, z: 4, core: 2. Of those that a mesh axis runs over, the one named last changes fastest.
Arguments:
- tokens: int32 [256, 768], P(('dp', 'fsdp'))
- grad_y: bfloat16 [256, 768, 768], P(('dp', 'fsdp'))
- embedding: bfloat16 [33, 768], P(None, 'fsdp')
- ln1_gain: bfloat16 [768], P('fsdp')
- ln1_bias: bfloat16 [768], P('fsdp')
- w_qkv: bfloat16 [768, 2304], P('fsdp')
- b_qkv: bfloat16 [2304], P('fsdp')
- w_out: bfloat16 [768, 768], P('fsdp')
- b_out: bfloat16 [768], P('fsdp')
- ln2_gain: bfloat16 [768], P('fsdp')
- ln2_bias: bfloat16 [768], P('fsdp')
- w_fc1: bfloat16 [768, 3072], P('fsdp')
- b_fc1: bfloat16 [3072], P('fsdp')
- w_fc2: bfloat16 [3072, 768], P('fsdp')
- b_fc2: bfloat16 [768], P('fsdp')
Outputs:
- output 1: bfloat16 [256, 768, 768], P(('dp', 'fsdp'))
- output 2: float32 [33, 768], P(None, 'fsdp')
- output 3: float32 [768], P('fsdp')
- output 4: float32 [768], P('fsdp')
- output 5: float32 [768, 2304], P('fsdp')
- output 6: float32 [2304], P('fsdp')
- output 7: float32 [768, 768], P('fsdp')
- output 8: float32 [768], P('fsdp')
- output 9: float32 [768], P('fsdp')
- output 10: float32 [768], P('fsdp')
- output 11: float32 [768, 3072], P('fsdp')
- output 12: float32 [3072], P('fsdp')
- output 13: float32 [3072, 768], P('fsdp')
- output 14: float32 [768], P('fsdp')
All inputs are finite; a program needn't handle non-finite values.
Results may differ from a plain program's by a relative error of at most 0.0118225.
Values are sent between devices in bfloat16 or wider.
A program may use at most 1 GiB of HBM per device.

v0:
```python
import functools
import jax
import jax.numpy as jnp
from jax import lax
from jax.sharding import PartitionSpec as P

HEAD_DIM = 64
MASK_ID = 32
PAD_ID = 1
MASK_RATIO = 0.15 * 0.8
LN_EPS = 1e-5
ROPE_BASE = 10000.0


def f32_einsum(form, lhs, rhs):
    return jnp.einsum(form, lhs, rhs, preferred_element_type=jnp.float32)


def norm_fwd(x_val, gain, bias):
    centered = x_val - jnp.mean(x_val, axis=-1, keepdims=True)
    inv_std = lax.rsqrt(jnp.mean(centered * centered, axis=-1, keepdims=True) + LN_EPS)
    x_hat = centered * inv_std
    return x_hat * gain.astype(jnp.float32) + bias.astype(jnp.float32), x_hat, inv_std


def norm_bwd(d_out, x_hat, inv_std, gain):
    d_hat = d_out * gain.astype(jnp.float32)
    d_x = inv_std * (d_hat - jnp.mean(d_hat, axis=-1, keepdims=True)
                     - x_hat * jnp.mean(d_hat * x_hat, axis=-1, keepdims=True))
    return d_x, jnp.sum(d_out * x_hat, axis=(0, 1)), jnp.sum(d_out, axis=(0, 1))


def rope_tables(seq_len):
    inv_freq = 1.0 / (ROPE_BASE ** (jnp.arange(0, HEAD_DIM, 2, dtype=jnp.float32) / HEAD_DIM))
    angles = jnp.arange(seq_len, dtype=jnp.float32)[:, None] * inv_freq[None, :]
    return jnp.cos(angles)[:, None, :], jnp.sin(angles)[:, None, :]


def rotate(x_val, cos_tab, sin_tab):
    half_dim = x_val.shape[-1] // 2
    low_half = x_val[..., :half_dim]
    high_half = x_val[..., half_dim:]
    return jnp.concatenate([low_half * cos_tab - high_half * sin_tab, high_half * cos_tab + low_half * sin_tab], axis=-1)


def layer_step(tokens, grad_y, weights):
    (embedding, ln1_gain, ln1_bias, w_qkv, b_qkv, w_out, b_out,
     ln2_gain, ln2_bias, w_fc1, b_fc1, w_fc2, b_fc2) = weights
    batch_rows, seq_len = tokens.shape
    vocab_size, model_dim = embedding.shape
    num_heads = model_dim // HEAD_DIM
    one_hot = tokens[:, :, None] == jnp.arange(vocab_size)[None, None, :]
    is_mask = tokens == MASK_ID
    is_pad = tokens == PAD_ID
    mask_count = jnp.sum(is_mask, axis=1).astype(jnp.float32)
    real_count = jnp.sum(jnp.logical_not(is_pad), axis=1).astype(jnp.float32)
    factor = (1.0 - MASK_RATIO) / (1.0 - mask_count / real_count)
    keep_scale = jnp.where(is_mask | is_pad, 0.0, factor[:, None])[:, :, None]
    looked_up = f32_einsum('blv,vd->bld', one_hot.astype(jnp.bfloat16), embedding)
    x_res = (looked_up * keep_scale).astype(jnp.bfloat16).astype(jnp.float32)
    norm_one, hat_one, inv_one = norm_fwd(x_res, ln1_gain, ln1_bias)
    h_one = norm_one.astype(jnp.bfloat16)
    qkv_proj = f32_einsum('bld,de->ble', h_one, w_qkv) + b_qkv.astype(jnp.float32)
    qkv_proj = qkv_proj.reshape(batch_rows, seq_len, 3, num_heads, HEAD_DIM)
    cos_tab, sin_tab = rope_tables(seq_len)
    queries = rotate(qkv_proj[:, :, 0] * HEAD_DIM ** -0.5, cos_tab, sin_tab).astype(jnp.bfloat16)
    key_rows = rotate(qkv_proj[:, :, 1], cos_tab, sin_tab).astype(jnp.bfloat16)
    values = qkv_proj[:, :, 2].astype(jnp.bfloat16)
    scores = f32_einsum('bqhd,bkhd->bhqk', queries, key_rows)
    scores = jnp.where(is_pad[:, None, None, :], -1e30, scores)
    attn_prob = jax.nn.softmax(scores, axis=-1)
    prob_b16 = attn_prob.astype(jnp.bfloat16)
    context = f32_einsum('bhqk,bkhd->bqhd', prob_b16, values).astype(jnp.bfloat16)
    context = context.reshape(batch_rows, seq_len, model_dim)
    x_mid = x_res + f32_einsum('bld,de->ble', context, w_out) + b_out.astype(jnp.float32)
    norm_two, hat_two, inv_two = norm_fwd(x_mid, ln2_gain, ln2_bias)
    h_two = norm_two.astype(jnp.bfloat16)
    pre_act = f32_einsum('bld,df->blf', h_two, w_fc1) + b_fc1.astype(jnp.float32)
    hidden_act, gelu_pull = jax.vjp(functools.partial(jax.nn.gelu, approximate=False), pre_act)
    act_b16 = hidden_act.astype(jnp.bfloat16)
    hidden = (x_mid + f32_einsum('blf,fd->bld', act_b16, w_fc2) + b_fc2.astype(jnp.float32)).astype(jnp.bfloat16)

    grad_res = grad_y.astype(jnp.float32)
    g_b_fc2 = jnp.sum(grad_res, axis=(0, 1))
    g_w_fc2 = f32_einsum('blf,bld->fd', act_b16, grad_y)
    d_pre = gelu_pull(f32_einsum('bld,fd->blf', grad_y, w_fc2))[0]
    g_b_fc1 = jnp.sum(d_pre, axis=(0, 1))
    d_pre = d_pre.astype(jnp.bfloat16)
    g_w_fc1 = f32_einsum('bld,blf->df', h_two, d_pre)
    d_two, g_ln2_gain, g_ln2_bias = norm_bwd(f32_einsum('blf,df->bld', d_pre, w_fc1), hat_two, inv_two, ln2_gain)
    d_mid = grad_res + d_two
    g_b_out = jnp.sum(d_mid, axis=(0, 1))
    d_mid_b16 = d_mid.astype(jnp.bfloat16)
    g_w_out = f32_einsum('bld,ble->de', context, d_mid_b16)
    d_ctx = f32_einsum('ble,de->bld', d_mid_b16, w_out).astype(jnp.bfloat16)
    d_ctx = d_ctx.reshape(batch_rows, seq_len, num_heads, HEAD_DIM)
    d_prob = f32_einsum('bqhd,bkhd->bhqk', d_ctx, values)
    d_val = f32_einsum('bhqk,bqhd->bkhd', prob_b16, d_ctx)
    d_scores = attn_prob * (d_prob - jnp.sum(d_prob * attn_prob, axis=-1, keepdims=True))
    d_scores = d_scores.astype(jnp.bfloat16)
    d_query = rotate(f32_einsum('bhqk,bkhd->bqhd', d_scores, key_rows), cos_tab, -sin_tab) * HEAD_DIM ** -0.5
    d_key = rotate(f32_einsum('bhqk,bqhd->bkhd', d_scores, queries), cos_tab, -sin_tab)
    d_qkv = jnp.stack([d_query, d_key, d_val], axis=2).reshape(batch_rows, seq_len, 3 * model_dim)
    g_b_qkv = jnp.sum(d_qkv, axis=(0, 1))
    d_qkv = d_qkv.astype(jnp.bfloat16)
    g_w_qkv = f32_einsum('bld,ble->de', h_one, d_qkv)
    d_one, g_ln1_gain, g_ln1_bias = norm_bwd(f32_einsum('ble,de->bld', d_qkv, w_qkv), hat_one, inv_one, ln1_gain)
    d_in = d_mid + d_one
    g_embedding = f32_einsum('blv,bld->vd', one_hot.astype(jnp.float32), d_in * keep_scale)
    full_grads = (g_embedding, g_ln1_gain, g_ln1_bias, g_w_qkv, g_b_qkv, g_w_out, g_b_out,
                  g_ln2_gain, g_ln2_bias, g_w_fc1, g_b_fc1, g_w_fc2, g_b_fc2)
    return hidden, full_grads


def solution(mesh):
    row_spec = P(('dp', 'fsdp'), None)
    act_spec = P(('dp', 'fsdp'), None, None)
    param_specs = (P(None, 'fsdp'),) + (P('fsdp'),) * 12

    def local_step(tokens, grad_y, *shards):
        full_params = [lax.all_gather(shards[0], 'fsdp', axis=1, tiled=True)]
        full_params += [lax.all_gather(shard, 'fsdp', axis=0, tiled=True) for shard in shards[1:]]
        hidden, full_grads = layer_step(tokens, grad_y, full_params)
        grad_parts = [lax.psum(lax.psum_scatter(full_grads[0], 'fsdp', scatter_dimension=1, tiled=True), 'dp')]
        grad_parts += [lax.psum(lax.psum_scatter(full_grad, 'fsdp', scatter_dimension=0, tiled=True), 'dp')
                       for full_grad in full_grads[1:]]
        return (hidden,) + tuple(grad_parts)

    return jax.shard_map(local_step, mesh=mesh, in_specs=(row_spec, act_spec) + param_specs,
                         out_specs=(act_spec,) + param_specs, check_vma=False)
```

profile of v0, /device:TPU:0, one launch (start us, length us, event | category | flops | bytes accessed | tf_op | source)
XLA Modules:
  0.0 893.2 jit_solution(15421339618648699187)
XLA Ops:
  31.2 4.5 copy.89
  35.7 11.3 %convolution_add_fusion = f32[2,768,2304]{2,1,0:T(8,128)} fusion(f32[2304]{0:T(1024)S(1)} %reshape.223, bf16[768,2304]{1,0:T(8,128)(2,1)} %all-gather.13.cloned.1.call-done, bf16[2,768,768]{1,2,0:T(8,128)(2,1)S(1)} %get-tuple-element.110, f32[768]{0:T(1024)S(1)} %reshape.222, f32[768]{0:T(1024)S(1)} %reshape.221, f32[2,768]{1,0:T(2,128)S(1)} %add_rsqrt_fusion.1, ...), kind=kOutput, calls=%fused_computation.38 | convolution fusion | flops 5446434816 | bytes 20081664 | tf_op jit(solution)/shard_map/bld,de->ble/dot_general | solution.py:16
  47.0 15.1 %copy.80 = f32[2,768,2304]{1,2,0:T(8,128)} copy(f32[2,768,2304]{2,1,0:T(8,128)} %convolution_add_fusion) | data formatting | bytes 28311552 | tf_op jit(solution)/shard_map/add | solution.py:63
  62.2 7.1 fusion.98
  75.6 26.2 %fusion.99 = (f32[2,12,768]{2,1,0:T(8,128)}, f32[2,12,768,768]{2,3,1,0:T(8,128)}) fusion(pred[2,768]{1,0:T(4,128)(4,1)} %broadcast_compare_fusion, bf16[2,768,12,32]{1,3,2,0:T(8,128)(2,1)S(1)} %get-tuple-element.104, bf16[2,768,12,32]{1,3,2,0:T(8,128)(2,1)} %get-tuple-element.105, bf16[2,768,12,32]{1,3,2,0:T(8,128)(2,1)} %get-tuple-element.98, ...), kind=kOutput, calls=%fused_computation.163 | convolution fusion | flops 1863844608 | bytes 61416960 | tf_op jit(solution)/shard_map/sub | solution.py:71
  101.8 22.2 %fusion.66 = bf16[2,12,64,768]{3,2,1,0:T(8,128)(2,1)} fusion(f32[2,12,768,768]{2,3,1,0:T(8,128)} %get-tuple-element.112, f32[2,12,768]{2,1,0:T(8,128)} %get-tuple-element.111, f32[2,768,3,12,64]{1,4,3,2,0:T(8,128)} %bitcast.97), kind=kOutput, calls=%fused_computation.114 | convolution fusion | flops 1841430528 | bytes 61440000 | tf_op jit(solution)/shard_map/bhqk,bkhd->bqhd/dot_general | solution.py:16
  130.9 24.0 %fusion.49 = (u8[768,3072]{1,0:T(8,128)(4,1)S(1)}, u8[768,3072]{1,0:T(8,128)(4,1)}, f32[2,768,3072]{2,1,0:T(8,128)}) fusion(f32[3072]{0:T(1024)S(1)} %bitcast.107, bf16[768,3072]{1,0:T(8,128)(2,1)} %all-gather.17.cloned.1.call-done, f32[2,768,768]{1,2,0:T(8,128)} %copy-done, f32[768]{0:T(1024)S(1)} %copy-done.43, f32[768]{0:T(1024)S(1)} %reshape.225, ...), kind=kOutput, calls=%fused_computation.86 | convolution fusion | flops 7314997248 | bytes 33060864 | tf_op jit(solution)/shard_map/bld,df->blf/dot_general | solution.py:16
  155.0 47.1 %multiply_convert_fusion.1 = (bf16[2,768,3072]{2,1,0:T(8,128)(2,1)}, f32[2,768,3072]{2,1,0:T(8,128)}) fusion(f32[2,768,3072]{2,1,0:T(8,128)} %get-tuple-element.115, f32[3072]{0:T(1024)S(1)} %bitcast.108, u8[768,3072]{1,0:T(8,128)(4,1)} %get-tuple-element.57, u8[768,3072]{1,0:T(8,128)(4,1)S(1)} %get-tuple-element.56), kind=kLoop, calls=%fused_computation.17 | loop fusion | flops 335020032 | bytes 51916800 | tf_op jit(solution)/shard_map/convert_element_type | solution.py:80
  202.1 26.8 %fusion.103 = (f32[3072]{0:T(1024)}, bf16[2,768,3072]{2,1,0:T(8,128)(2,1)}) fusion(f32[2,768,3072]{2,1,0:T(8,128)} %get-tuple-element.90, bf16[2,768,768]{2,1,0:T(8,128)(2,1)} %param.16, bf16[3072,768]{1,0:T(8,128)(2,1)} %all-gather.19.cloned.1.call-done, f32[2,768,3072]{2,1,0:T(8,128)} %get-tuple-element.115, f32[3072]{0:T(1024)S(1)} %bitcast.109), kind=kOutput, calls=%fused_computation.167 | convolution fusion | flops 7323251712 | bytes 54288384 | tf_op jit(solution)/shard_map/bld,fd->blf/dot_general | solution.py:16
  228.9 12.1 %fusion.102 = (f32[768]{0:T(1024)}, f32[2,768,768]{2,1,0:T(8,128)}) fusion(bf16[768,3072]{1,0:T(8,128)(2,1)S(1)} %bitcast.111, bf16[2,768,3072]{2,1,0:T(8,128)(2,1)} %get-tuple-element.123), kind=kOutput, calls=%fused_computation.166 | convolution fusion | flops 7248935936 | bytes 18877440 | tf_op jit(solution)/shard_map/blf,df->bld/dot_general | solution.py:16
  241.0 6.3 copy.90
  247.3 5.4 multiply_reduce_fusion.1
  259.2 22.5 %fusion.63 = f32[2,768,1,12,64]{1,4,3,0,2:T(8,128)} fusion(bf16[2,768,12,64]{1,3,2,0:T(8,128)(2,1)S(1)} %bitcast.114, f32[2,12,768,768]{2,3,1,0:T(8,128)} %get-tuple-element.112, f32[2,12,768]{2,1,0:T(8,128)S(1)} %copy-done.20), kind=kOutput, calls=%fused_computation.113 | convolution fusion | flops 1840250880 | bytes 63774720 | tf_op jit(solution)/shard_map/bhqk,bqhd->bkhd/dot_general | solution.py:16
  281.8 38.1 %multiply_reduce_fusion = (f32[2,12,768]{2,1,0:T(8,128)S(1)}, f32[2,12,768,768]{2,3,1,0:T(8,128)}) fusion(f32[2,12,768,768]{2,3,1,0:T(8,128)} %get-tuple-element.112, f32[2,12,768]{2,1,0:T(8,128)S(1)} %copy-done.20, bf16[2,768,12,64]{1,3,2,0:T(8,128)(2,1)S(1)} %bitcast.115, f32[2,768,3,12,64]{1,4,3,2,0:T(8,128)} %bitcast.98), kind=kOutput, calls=%fused_computation.2 | convolution fusion | flops 1854388224 | bytes 118112256 | tf_op jit(solution)/shard_map/bqhd,bkhd->bhqk/dot_general | solution.py:16
  319.8 44.7 %multiply_convert_fusion = bf16[2,12,768,768]{2,3,1,0:T(8,128)(2,1)} fusion(f32[2,12,768,768]{2,3,1,0:T(8,128)} %get-tuple-element.117, f32[2,12,768]{2,1,0:T(8,128)S(1)} %get-tuple-element.116, f32[2,12,768,768]{2,3,1,0:T(8,128)} %get-tuple-element.112, f32[2,12,768]{2,1,0:T(8,128)S(1)} %copy-done.20), kind=kLoop, calls=%fused_computation.1 | loop fusion | flops 56623104 | bytes 141705216 | tf_op jit(solution)/shard_map/convert_element_type | solution.py:100
  364.5 14.3 %convolution_bitcast_fusion.3 = f32[2,768,12,64]{1,3,2,0:T(8,128)S(1)} fusion(bf16[2,12,768,768]{2,3,1,0:T(8,128)(2,1)} %multiply_convert_fusion, bf16[2,768,12,32]{1,3,2,0:T(8,128)(2,1)} %get-tuple-element.98, bf16[2,768,12,32]{1,3,2,0:T(8,128)(2,1)} %get-tuple-element.97), kind=kOutput, calls=%fused_computation.111 | convolution fusion | flops 1816657920 | bytes 35389440 | tf_op jit(solution)/shard_map/bhqk,bqhd->bkhd/dot_general | solution.py:16
  378.8 16.6 %convolution_bitcast_fusion.4 = f32[2,768,12,64]{1,3,2,0:T(8,128)} fusion(bf16[2,12,768,768]{2,3,1,0:T(8,128)(2,1)} %multiply_convert_fusion, bf16[2,768,12,32]{1,3,2,0:T(8,128)(2,1)S(1)} %copy-done.11, bf16[2,768,12,32]{1,3,2,0:T(8,128)(2,1)} %get-tuple-element.105), kind=kOutput, calls=%fused_computation.112 | convolution fusion | flops 1816657920 | bytes 35389440 | tf_op jit(solution)/shard_map/bhqk,bkhd->bqhd/dot_general | solution.py:16
  406.6 12.0 %fusion.101 = (f32[768]{0:T(1024)S(1)}, f32[2,768,768]{2,1,0:T(8,128)}) fusion(bf16[2,768,2304]{1,2,0:T(8,128)(2,1)S(1)} %bitcast.101, bf16[768,2304]{1,0:T(8,128)(2,1)} %all-gather.13.cloned.1.call-done), kind=kOutput, calls=%fused_computation.165 | convolution fusion | flops 5436996608 | bytes 15338496 | tf_op jit(solution)/shard_map/ble,de->bld/dot_general | solution.py:16
  418.6 6.2 copy.98
  424.9 4.2 fusion.33
  429.2 4.9 fusion.73
  434.1 6.5 convolution_bitcast_fusion.5
  440.7 11.3 %convolution_bitcast_fusion.1 = f32[768,2304]{1,0:T(8,128)} fusion(bf16[2,768,2304]{1,2,0:T(8,128)(2,1)} %bitcast.102, bf16[2,768,768]{1,2,0:T(8,128)(2,1)S(1)} %copy-done.6, f32[768]{0:T(1024)S(1)} %copy-done.46, f32[768]{0:T(1024)S(1)} %copy-done.30, f32[2,768]{1,0:T(2,128)S(1)} %copy-done.28, f32[2,768]{1,0:T(2,128)S(1)} %copy-done.22), kind=kOutput, calls=%fused_computation.45 | convolution fusion | flops 5442895872 | bytes 16533504 | tf_op jit(solution)/shard_map/bld,ble->de/dot_general | solution.py:16
  453.6 12.3 %convolution_bitcast_fusion = f32[3072,768]{1,0:T(8,128)} fusion(bf16[2,768,3072]{2,1,0:T(8,128)(2,1)} %get-tuple-element.89, bf16[2,768,768]{2,1,0:T(8,128)(2,1)S(1)} %copy-done.12), kind=kOutput, calls=%fused_computation.44 | convolution fusion | flops 7247757312 | bytes 21233664 | tf_op jit(solution)/shard_map/blf,bld->fd/dot_general | solution.py:16
  466.7 14.7 %convolution_bitcast_fusion.2 = f32[768,3072]{1,0:T(8,128)} fusion(bf16[2,768,3072]{2,1,0:T(8,128)(2,1)} %get-tuple-element.123, f32[2,768,768]{1,2,0:T(8,128)} %copy-done, f32[768]{0:T(1024)S(1)} %copy-done.44, f32[768]{0:T(1024)S(1)} %copy-done.32, f32[2,768]{1,0:T(2,128)S(1)} %copy-done.26, f32[2,768]{1,0:T(2,128)S(1)} %copy-done.19), kind=kOutput, calls=%fused_computation.46 | convolution fusion | flops 7253655552 | bytes 23611392 | tf_op jit(solution)/shard_map/bld,blf->df/dot_general | solution.py:16
  484.6 5.7 fusion.18
  499.3 6.9 reduce-scatter.14.cloned.1.call-done
  506.3 23.1 %reduce-scatter.12.cloned.1.call-done = f32[384,3072]{1,0:T(8,128)} async-done(((f32[768,3072]{1,0:T(8,128)}), f32[384,3072]{1,0:T(8,128)}) %reduce-scatter.12.cloned.1.call-update) | async-done | bytes 4718608 | tf_op jit(solution)/shard_map/reduce_scatter | solution.py:125
  531.9 12.3 %add_convert_fusion = bf16[2,768,768]{1,2,0:T(8,128)(2,1)S(1)} fusion(f32[2,768,768]{1,2,0:T(8,128)} %copy-done, f32[768]{0:T(1024)S(1)} %reshape.228, bf16[2,768,3072]{2,1,0:T(8,128)(2,1)} %get-tuple-element.89, bf16[3072,768]{1,0:T(8,128)(2,1)} %all-gather.19.cloned.1.call-done), kind=kOutput, calls=%fused_computation.80 | convolution fusion | flops 7251296256 | bytes 21236736 | tf_op jit(solution)/shard_map/blf,fd->bld/dot_general | solution.py:16
  546.7 122.8 %all-reduce.14.cloned.1.call-done = (f32[33,384]{1,0:T(8,128)}, f32[384]{0:T(512)}, f32[384]{0:T(512)}, f32[1152]{0:T(1024)}, f32[384]{0:T(512)}, /*index=5*/f32...) async-done(((f32[33,384]{1,0:T(8,128)}, f32[384]{0:T(512)}, f32[384]{0:T(512)}, f32[1152]{0:T(1024)}, f32[384]{0:T(512)}, /*index=5*/f32[384]{0:T(512)}, f32[384]{0:T(512)}, ...) | async-done | bytes 70672 | tf_op jit(solution)/shard_map/psum | solution.py:124
  669.5 199.8 %all-reduce.16.cloned.1.call-done = (f32[384,2304]{1,0:T(8,128)}, f32[384,768]{1,0:T(8,128)}, f32[384,3072]{1,0:T(8,128)}, f32[1536,768]{1,0:T(8,128)}) async-done(((f32[384,2304]{1,0:T(8,128)}, f32[384,768]{1,0:T(8,128)}, f32[384,3072]{1,0:T(8,128)}, f32[1536,768]{1,0:T(8,128)}), (f32[384,2304]{1,0:T(8,128)}, f32[384,768]{1,0:T(8,128)}, f32[384,3072]{1,0:T(8,128)}, ...) | async-done | bytes 14155792 | tf_op jit(solution)/shard_map/psum | solution.py:125
  873.5 4.1 copy.152
  (262 shorter events, 85.4 us)
Async XLA Ops:
  7.2 13.1 %copy-start.58 = (bf16[384]{0:T(512)(128)(2,1)S(1)}, bf16[384]{0:T(512)(128)(2,1)}, u32[]{:S(2)}) copy-start(bf16[384]{0:T(512)(128)(2,1)} %param.25) | copy-start | bytes 2308
  7.2 15.6 %copy-start.48 = (bf16[1152]{0:T(1024)(128)(2,1)S(1)}, bf16[1152]{0:T(1024)(128)(2,1)}, u32[]{:S(2)}) copy-start(bf16[1152]{0:T(1024)(128)(2,1)} %param.21) | copy-start | bytes 6916
  7.3 17.6 %copy-start.49 = (bf16[1536]{0:T(1024)(128)(2,1)S(1)}, bf16[1536]{0:T(1024)(128)(2,1)}, u32[]{:S(2)}) copy-start(bf16[1536]{0:T(1024)(128)(2,1)} %param.27) | copy-start | bytes 9220
  7.3 19.4 %copy-start.33 = (bf16[33,384]{1,0:T(8,128)(2,1)S(1)}, bf16[33,384]{1,0:T(8,128)(2,1)}, u32[]{:S(2)}) copy-start(bf16[33,384]{1,0:T(8,128)(2,1)} %param.17) | copy-start | bytes 76036
  7.3 28.4 %all-gather.13.cloned.1.call-start = ((), (), s32[]{:S(2)}) async-start(), calls=%async_computation.5 | async-start | bytes 5308416 | tf_op jit(solution)/shard_map/all_gather | solution.py:122
  8.0 116.1 %all-gather.15.cloned.1.call-start = ((), (), s32[]{:S(2)}) async-start(), calls=%async_computation.6 | async-start | bytes 1769472 | tf_op jit(solution)/shard_map/all_gather | solution.py:122
  10.2 120.7 %all-gather.17.cloned.1.call-start = ((), (), s32[]{:S(2)}) async-start(), calls=%async_computation.7 | async-start | bytes 7077888 | tf_op jit(solution)/shard_map/all_gather | solution.py:122
  10.9 191.1 %all-gather.19.cloned.1.call-start = ((), (), s32[]{:S(2)}) async-start(), calls=%async_computation.8 | async-start | bytes 7077888 | tf_op jit(solution)/shard_map/all_gather | solution.py:122
  11.5 487.7 %reduce-scatter.6.cloned.1.call-start = ((), (), s32[]{:S(2)}) async-start(), calls=%async_computation.9 | async-start | bytes 184320 | tf_op jit(solution)/shard_map/reduce_scatter | solution.py:124
  14.2 21.5 %copy-start.29 = (f32[768]{0:T(1024)}, f32[768]{0:T(1024)S(1)}, u32[]{:S(2)}) copy-start(f32[768]{0:T(1024)S(1)} %reshape.221) | copy-start | bytes 9220
  16.1 19.6 %copy-start.45 = (f32[768]{0:T(1024)}, f32[768]{0:T(1024)S(1)}, u32[]{:S(2)}) copy-start(f32[768]{0:T(1024)S(1)} %reshape.222) | copy-start | bytes 9220
  20.4 232.3 %copy-start.31 = (f32[768]{0:T(1024)}, f32[768]{0:T(1024)S(1)}, u32[]{:S(2)}) copy-start(f32[768]{0:T(1024)S(1)} %reshape.225) | copy-start | bytes 9220
  30.5 93.6 %copy-start.5 = (bf16[2,768,768]{1,2,0:T(8,128)(2,1)}, bf16[2,768,768]{1,2,0:T(8,128)(2,1)S(1)}, u32[]{:S(2)}) copy-start(bf16[2,768,768]{1,2,0:T(8,128)(2,1)S(1)} %get-tuple-element.110) | copy-start | bytes 7077892
  30.5 16.5 %copy-start.21 = (f32[2,768]{1,0:T(2,128)}, f32[2,768]{1,0:T(2,128)S(1)}, u32[]{:S(2)}) copy-start(f32[2,768]{1,0:T(2,128)S(1)} %broadcast_multiply_fusion.5) | copy-start | bytes 18436
  31.2 15.8 %copy-start.27 = (f32[2,768]{1,0:T(2,128)}, f32[2,768]{1,0:T(2,128)S(1)}, u32[]{:S(2)}) copy-start(f32[2,768]{1,0:T(2,128)S(1)} %add_rsqrt_fusion.1) | copy-start | bytes 18436
  75.6 26.2 %copy-start.10 = (bf16[2,768,12,32]{1,3,2,0:T(8,128)(2,1)}, bf16[2,768,12,32]{1,3,2,0:T(8,128)(2,1)S(1)}, u32[]{:S(2)}) copy-start(bf16[2,768,12,32]{1,3,2,0:T(8,128)(2,1)S(1)} %get-tuple-element.104) | copy-start | bytes 3538948
  101.8 22.3 %copy-start.47 = (f32[768]{0:T(1024)S(1)}, f32[768]{0:T(1024)}, u32[]{:S(2)}) copy-start(f32[768]{0:T(1024)} %reshape.224) | copy-start | bytes 9220
  128.2 124.5 %copy-start.18 = (f32[2,768]{1,0:T(2,128)}, f32[2,768]{1,0:T(2,128)S(1)}, u32[]{:S(2)}) copy-start(f32[2,768]{1,0:T(2,128)S(1)} %broadcast_multiply_fusion.4) | copy-start | bytes 18436
  130.9 121.9 %copy-start.25 = (f32[2,768]{1,0:T(2,128)}, f32[2,768]{1,0:T(2,128)S(1)}, u32[]{:S(2)}) copy-start(f32[2,768]{1,0:T(2,128)S(1)} %add_rsqrt_fusion) | copy-start | bytes 18436
  155.0 73.9 %slice-start.8 = ((s8[4718592]{0:T(1024)(128)(4,1)}), s8[524288]{0:T(1024)(128)(4,1)S(1)}, s32[]{:S(2)}) async-start(s8[4718592]{0:T(1024)(128)(4,1)} %bitcast.110), calls=%async_computation.24 | async-start | bytes 1048576
  202.1 26.8 %slice-start.9 = ((s8[4718592]{0:T(1024)(128)(4,1)}), s8[4194304]{0:T(1024)(128)(4,1)S(1)}, s32[]{:S(2)}) async-start(s8[4718592]{0:T(1024)(128)(4,1)} %bitcast.110), calls=%async_computation.25 | async-start | bytes 8388608
  364.5 14.3 %copy-start.11 = (bf16[2,768,12,32]{1,3,2,0:T(8,128)(2,1)S(1)}, bf16[2,768,12,32]{1,3,2,0:T(8,128)(2,1)}, u32[]{:S(2)}) copy-start(bf16[2,768,12,32]{1,3,2,0:T(8,128)(2,1)} %copy-done.10) | copy-start | bytes 3538948
  378.8 16.6 %copy-start.15 = (f32[768,32]{0,1:T(8,128)S(1)}, f32[768,32]{0,1:T(8,128)}, u32[]{:S(2)}) copy-start(f32[768,32]{0,1:T(8,128)} %get-tuple-element.108) | copy-start | bytes 294916
  378.8 16.6 %copy-start.16 = (f32[768,32]{0,1:T(8,128)S(1)}, f32[768,32]{0,1:T(8,128)}, u32[]{:S(2)}) copy-start(f32[768,32]{0,1:T(8,128)} %get-tuple-element.106) | copy-start | bytes 294916
  406.6 12.0 %copy-start.9 = (bf16[2,768,3,12,64]{1,4,3,2,0:T(8,128)(2,1)}, bf16[2,768,3,12,64]{1,4,3,2,0:T(8,128)(2,1)S(1)}, u32[]{:S(2)}) copy-start(bf16[2,768,3,12,64]{1,4,3,2,0:T(8,128)(2,1)S(1)} %copy.96) | copy-start | bytes 21233668
  434.1 65.2 %reduce-scatter.10.cloned.1.call-start = ((), (), s32[]{:S(2)}) async-start(), calls=%async_computation.11 | async-start | bytes 3538944 | tf_op jit(solution)/shard_map/reduce_scatter | solution.py:125
  440.6 58.7 %reduce-scatter.8.cloned.1.call-start = ((), (), s32[]{:S(2)}) async-start(), calls=%async_computation.10 | async-start | bytes 10616832 | tf_op jit(solution)/shard_map/reduce_scatter | solution.py:125
  452.0 54.3 %reduce-scatter.14.cloned.1.call-start = ((), (), s32[]{:S(2)}) async-start(), calls=%async_computation.13 | async-start | bytes 14155776 | tf_op jit(solution)/shard_map/reduce_scatter | solution.py:125
  466.0 63.4 %reduce-scatter.12.cloned.1.call-start = ((), (), s32[]{:S(2)}) async-start(), calls=%async_computation.12 | async-start | bytes 14155776 | tf_op jit(solution)/shard_map/reduce_scatter | solution.py:125
  481.4 188.1 %all-reduce.14.cloned.1.call-start = ((), (), s32[]{:S(2)}) async-start(), calls=%async_computation.14 | async-start | bytes 180224 | tf_op jit(solution)/shard_map/psum | solution.py:124
  499.2 370.0 %all-reduce.16.cloned.1.call-start = ((), (), s32[]{:S(2)}) async-start(), calls=%async_computation.15 | async-start | bytes 28311552 | tf_op jit(solution)/shard_map/psum | solution.py:125
  669.5 208.1 %copy-start.41 = (f32[1152]{0:T(1024)S(1)}, f32[1152]{0:T(1024)}, u32[]{:S(2)}) copy-start(f32[1152]{0:T(1024)} %get-tuple-element.133) | copy-start | bytes 13828
  (51 other events, 252.8 us)
Sparse Core Ops, SparseCore 0:
  9.7 18.1 all-gather.12
  30.1 13.1 all-gather.14
  45.0 18.8 all-gather.16
  65.4 18.8 all-gather.18
  434.2 12.5 reduce-scatter.5
  449.6 13.5 reduce-scatter.9
  465.5 17.6 reduce-scatter.7
  485.6 20.6 reduce-scatter.13
  508.7 20.5 reduce-scatter.11
  536.5 132.9 all-reduce.13
  675.6 193.5 all-reduce.15
where the time goes:
time: 897 us; the launch traced here: 893 us
  waiting for transfers between devices  355 us (40%)
  matrix products  295 us (33%)
  other arithmetic  126 us (14%)
  local copies, waits for them, and re-layouts  80.1 us (9%)
  blocking collectives  20 us (2%)
  between operations  16.9 us (2%)
    dot_general x19, matrix products, f32_einsum(): return jnp.einsum(form, lhs, rhs, preferred_element_type=jnp.float32)  269 us
    psum x1, waiting for transfers between devices, local_step(): lax.psum(lax.psum_scatter(full_grad, 'fsdp', scatter_dimension=0, tiled=T...  200 us
    psum x1, waiting for transfers between devices, local_step(): lax.psum(lax.psum_scatter(full_grads[0], 'fsdp', scatter_dimension=1, til...  123 us
    convert_element_type x1, other arithmetic, layer_step(): act_b16 = hidden_act.astype(jnp.bfloat16)  47.1 us
    convert_element_type x1, other arithmetic, layer_step(): d_scores = d_scores.astype(jnp.bfloat16)  44.7 us
    unnamed x177, local copies, waits for them, and re-layouts  43.2 us
    reduce_scatter x4, waiting for transfers between devices, local_step(): lax.psum_scatter(full_grad, 'fsdp', scatter_dimension=0, tiled=True)  30 us
    sub x1, matrix products, layer_step(): attn_prob = jax.nn.softmax(scores, axis=-1)  26.2 us
  transfers between devices with their start and end apart: 11, of which 4 were waited for; matrix products, arithmetic and copies ran while one was open for 28% of the time, Pallas kernels for 0%

commit v1 on v0

v1 whole, which is shorter than its diff:
```python
import functools
import jax
import jax.numpy as jnp
import numpy as np
from jax import lax
from jax.experimental import pallas as pl
from jax.experimental.pallas import tpu as pltpu
from jax.sharding import PartitionSpec as P

HEAD_DIM = 64
MASK_ID = 32
PAD_ID = 1
MASK_RATIO = 0.15 * 0.8
LN_EPS = 1e-5
ROPE_BASE = 10000.0
F32 = jnp.float32
BF16 = jnp.bfloat16
EMB_ROWS = 40
SMALL_ROWS = 64
VEC_ROW = 48
VECTORS = ('ln1_gain', 'ln1_bias', 'b_out', 'ln2_gain', 'ln2_bias', 'b_fc2', 'b_qkv', 'b_fc1')
VMEM_LIMIT = 60 << 20

NN = (((1,), (0,)), ((), ()))
NT = (((1,), (1,)), ((), ()))
TN = (((0,), (0,)), ((), ()))


def dot(lhs, rhs, dims=NN):
    return lax.dot_general(lhs, rhs, dims, preferred_element_type=F32)


def row_mean(x_val):
    return jnp.mean(x_val, axis=-1, keepdims=True)


def hat_of(x_val):
    centered = x_val - row_mean(x_val)
    inv_std = lax.rsqrt(row_mean(centered * centered) + LN_EPS)
    return centered * inv_std, inv_std


def hat_bwd(d_out, x_hat, inv_std, gain):
    d_hat = d_out * gain
    return inv_std * (d_hat - row_mean(d_hat)
                      - x_hat * row_mean(d_hat * x_hat))


def rope_tables(seq_len):
    power = np.arange(0, HEAD_DIM, 2, dtype=np.float32) / np.float32(HEAD_DIM)
    inv_freq = np.float32(1) / np.power(np.float32(ROPE_BASE), power)
    angles = np.outer(np.arange(seq_len, dtype=np.float32), inv_freq).astype(np.float64)
    cos, sin = np.cos(angles), np.sin(angles)
    return (jnp.asarray(np.concatenate([cos] * 4, axis=1), F32),
            jnp.asarray(np.concatenate([-sin, sin] * 2, axis=1), F32))


def col_sum(x_val):
    return jnp.sum(x_val, axis=0, keepdims=True)


def iota(shape, dim):
    return lax.broadcasted_iota(jnp.int32, shape, dim)


def vec_row(vec, name):
    at = VECTORS.index(name)
    count = {'b_qkv': 3, 'b_fc1': 4}.get(name, 1)
    row = VEC_ROW + at + (2 if name == 'b_fc1' else 0)
    return jnp.concatenate([vec[side, i:i + 1, :] for side in range(2) for i in range(row, row + count)],
                           axis=1).astype(F32)


def seq_counts(tok_row):
    masks = jnp.sum((tok_row == MASK_ID).astype(F32), axis=1, keepdims=True)
    real = jnp.sum((tok_row != PAD_ID).astype(F32), axis=1, keepdims=True)
    return (1.0 - MASK_RATIO) / (1.0 - masks / real), real


def live_one_hot(tok_row, rows):
    live = (tok_row == iota((rows, tok_row.shape[1]), 0)) & (tok_row != MASK_ID) & (tok_row != PAD_ID)
    return live.astype(F32).astype(BF16)


def swap_halves(x_val):
    low = (iota(x_val.shape, 1) & 32) == 0
    return jnp.where(low, pltpu.roll(x_val, 96, 1), pltpu.roll(x_val, 32, 1))


def rows_of_head(x_val, head):
    return jnp.where((iota(x_val.shape, 0) >= HEAD_DIM) == (head == 1), x_val, jnp.zeros_like(x_val))


def lanes_of_head(x_val, head):
    return jnp.where((iota(x_val.shape, 1) >= HEAD_DIM) == (head == 1), x_val, jnp.zeros_like(x_val))


def qkv_kernel(tok_seq, tok_tile, vec_part, cos, sin, wq_part, wo_part, w1_part, w2_part,
               x_out, q_out, k_out, v_out, vec_out, wq_out, wo_out, w1_out, w2_out,
               w_qkv, vec, wo_own, w1_own, w2_own, sends, recvs, local):
    step = pl.program_id(0)
    part = lax.axis_index('fsdp')
    partner = {'fsdp': 1 - part}
    dim = x_out.shape[1]

    def own_rows(ref):
        size = ref.shape[0] // 2
        return ref.at[pl.ds(part * size, size)]

    moves = [(wq_part, w_qkv), (vec_part, vec.at[part]), (wo_own, wo_out), (w1_own, w1_out), (w2_own, w2_out)]

    def target(n):
        return moves[n][1] if n == 1 else own_rows(moves[n][1])

    def remote(n):
        return pltpu.make_async_remote_copy(
            src_ref=moves[n][0], dst_ref=target(n), send_sem=sends.at[n], recv_sem=recvs.at[n],
            device_id=partner, device_id_type=MESH_ID)

    def keep_own(n):
        return pltpu.make_async_copy(moves[n][0], target(n), local.at[n])

    stage = ((wo_part, wo_own), (w1_part, w1_own), (w2_part, w2_own))

    def store_qkv():
        return pltpu.make_async_copy(w_qkv, wq_out, local.at[len(moves) + len(stage)])

    @pl.when(step == 0)
    def _():
        barrier = pltpu.get_barrier_semaphore()
        pl.semaphore_signal(barrier, inc=1, device_id=partner, device_id_type=MESH_ID)
        pl.semaphore_wait(barrier, 1)
        for n in range(2):
            remote(n).start()
            keep_own(n).start()
        loads = [pltpu.make_async_copy(src, dst, local.at[len(moves) + n]) for n, (src, dst) in enumerate(stage)]
        for copy in loads:
            copy.start()
        for n, copy in enumerate(loads):
            copy.wait()
            remote(n + 2).start()
            keep_own(n + 2).start()
        for n in range(2):
            remote(n).wait_recv()
            keep_own(n).wait()
        store_qkv().start()
        vec_out[...] = vec[...]

    scale, _ = seq_counts(tok_seq[0])
    emb = jnp.concatenate([vec[side, :VEC_ROW, :] for side in range(2)], axis=1)
    x_b16 = (dot(live_one_hot(tok_tile[0], VEC_ROW), emb, TN) * scale).astype(BF16)
    x_out[...] = x_b16
    x_hat, _ = hat_of(x_b16.astype(F32))
    h_one = (x_hat * vec_row(vec, 'ln1_gain') + vec_row(vec, 'ln1_bias')).astype(BF16)
    cos_tab, sin_tab = cos[...], sin[...]
    b_qkv = vec_row(vec, 'b_qkv')
    for index, out in enumerate((q_out, k_out, v_out)):
        cols = slice(index * dim, (index + 1) * dim)
        proj = dot(h_one, w_qkv[:, cols]) + b_qkv[:, cols]
        if out is v_out:
            out[...] = proj.astype(BF16)
            continue
        if out is q_out:
            proj = proj * HEAD_DIM ** -0.5
        for first in range(0, dim, PAIR):
            pair = slice(first, first + PAIR)
            z = proj[:, pair]
            out[:, pair] = (z * cos_tab + swap_halves(z) * sin_tab).astype(BF16)

    @pl.when(step == pl.num_programs(0) - 1)
    def _():
        store_qkv().wait()
        for n in range(len(moves)):
            remote(n).wait_send()
            if n >= 2:
                remote(n).wait_recv()
                keep_own(n).wait()


PAIR = 2 * HEAD_DIM
CHUNK = 256


def pad_bias(tok_row, keys):
    _, real = seq_counts(tok_row)
    return jnp.where(iota((keys, CHUNK), 0).astype(F32) < real, 0.0, -1e30)


def attn_fwd_kernel(q, k, v, tok_seq, ctx, lse):
    q_t = q[...].T
    v_t = v[...].T
    k_val = k[...]
    pad_tab = pad_bias(tok_seq[0], q.shape[0])
    for c in range(q.shape[0] // CHUNK):
        cols = slice(c * CHUNK, (c + 1) * CHUNK)
        parts = []
        for head in range(2):
            s_t = dot(k_val, rows_of_head(q_t[:, cols], head)) + pad_tab
            top = jnp.max(s_t, axis=0, keepdims=True)
            e_t = jnp.exp(s_t - top)
            total = col_sum(e_t)
            lse[0, head:head + 1, cols] = top + jnp.log(total)
            p_t = (e_t * (1.0 / total)).astype(BF16)
            parts.append(dot(v_t[head * HEAD_DIM:(head + 1) * HEAD_DIM, :], p_t))
        ctx[cols, :] = jnp.concatenate(parts, axis=0).T.astype(BF16)


def attn_bwd_kernel(q, k, v, d_ctx, lse, tok_seq, cos, sin, dq_out, dk_out, dv_out, sums, dk_acc, dv_acc):
    q_val, k_val, v_val, d_val = q[...], k[...], v[...], d_ctx[...]
    q_t, k_t, d_t = q_val.T, k_val.T, d_val.T
    pad_tab = pad_bias(tok_seq[0], q.shape[0])
    dq_sum = jnp.zeros((1, 128), F32)
    for c in range(q.shape[0] // CHUNK):
        cols = slice(c * CHUNK, (c + 1) * CHUNK)
        parts = []
        for head in range(2):
            s_t = dot(k_val, rows_of_head(q_t[:, cols], head)) + pad_tab
            p_t = jnp.exp(s_t - lse[0, head:head + 1, cols])
            dp_t = dot(v_val, rows_of_head(d_t[:, cols], head))
            delta = col_sum(p_t * dp_t)
            ds_t = (p_t * (dp_t - delta)).astype(BF16)
            dv_new = dot(p_t.astype(BF16), lanes_of_head(d_val[cols, :], head))
            dk_new = dot(ds_t, lanes_of_head(q_val[cols, :], head))
            if c == 0 and head == 0:
                dv_acc[...] = dv_new
                dk_acc[...] = dk_new
            else:
                dv_acc[...] += dv_new
                dk_acc[...] += dk_new
            parts.append(dot(k_t[head * HEAD_DIM:(head + 1) * HEAD_DIM, :], ds_t))
        z = jnp.concatenate(parts, axis=0).T
        z = (z * cos[cols, :] - swap_halves(z) * sin[cols, :]) * HEAD_DIM ** -0.5
        dq_sum = dq_sum + col_sum(z)
        dq_out[cols, :] = z.astype(BF16)
    z = dk_acc[...]
    z = z * cos[...] - swap_halves(z) * sin[...]
    dk_out[...] = z.astype(BF16)
    z_v = dv_acc[...]
    dv_out[...] = z_v.astype(BF16)
    sums[0] = jnp.concatenate([dq_sum, col_sum(z), col_sum(z_v)], axis=0)


FF_CHUNK = 768


def ffn_kernel(ctx, x_in, grad_y, w_out, w_fc1, w_fc2, vec,
               y_out, dmid_out, dctx_out, gw_out, gw_fc1, gw_fc2, g_small, g_b1, y_acc, dh_acc):
    step = pl.program_id(0)
    @pl.when(step == 0)
    def _():
        for ref in (gw_out, gw_fc1, gw_fc2, g_small, g_b1):
            ref[...] = jnp.zeros_like(ref)

    gain, b_fc1 = vec_row(vec, 'ln2_gain'), vec_row(vec, 'b_fc1')
    ctx_val = ctx[...]
    x_mid = x_in[...].astype(F32) + dot(ctx_val, w_out[...]) + vec_row(vec, 'b_out')
    x_hat, inv_std = hat_of(x_mid)
    h_two = (x_hat * gain + vec_row(vec, 'ln2_bias')).astype(BF16)
    dy = grad_y[...]
    y_acc[...] = x_mid + vec_row(vec, 'b_fc2')
    for j in range(w_fc1.shape[1] // FF_CHUNK):
        cols = slice(j * FF_CHUNK, (j + 1) * FF_CHUNK)
        pre = dot(h_two, w_fc1[:, cols]) + b_fc1[:, cols]
        cdf = 0.5 + 0.5 * lax.erf(pre * (0.5 ** 0.5))
        pdf = jnp.exp(pre * pre * -0.5) * 0.3989422804014327
        act = (pre * cdf).astype(BF16)
        d_act = dot(dy, w_fc2[cols, :], NT)
        d_pre = d_act * (cdf + pre * pdf)
        y_acc[...] += dot(act, w_fc2[cols, :])
        gw_fc2[cols, :] += dot(act, dy, TN)
        g_b1[:, cols] += col_sum(d_pre)
        d_pre = d_pre.astype(BF16)
        gw_fc1[j] += dot(h_two, d_pre, TN)
        d_h = dot(d_pre, w_fc1[:, cols], NT)
        if j == 0:
            dh_acc[...] = d_h
        else:
            dh_acc[...] += d_h
    y_out[...] = y_acc[...].astype(BF16)
    d_two = dh_acc[...]
    dy_f = dy.astype(F32)
    d_mid = dy_f + hat_bwd(d_two, x_hat, inv_std, gain)
    dmid_out[...] = d_mid
    for row, grad in enumerate((d_mid, d_two * x_hat, d_two, dy_f)):
        g_small[row:row + 1, :] += col_sum(grad)
    d_mid = d_mid.astype(BF16)
    gw_out[...] += dot(ctx_val, d_mid, TN)
    dctx_out[...] = dot(d_mid, w_out[...], NT).astype(BF16)


def whole(shape):
    return pl.BlockSpec(shape, lambda *_: (0,) * len(shape), pipeline_mode=pl.Buffered(1))


def shape_of(dims, dtype):
    return jax.ShapeDtypeStruct(dims, dtype)


def call(kernel, grid, in_specs, out_specs, out_shape, args, flops, scratch=(), name=None, collective_id=None):
    moved = sum(a.size * a.dtype.itemsize for a in args) + sum(o.size * o.dtype.itemsize for o in out_shape)
    return pl.pallas_call(
        kernel, grid=grid, in_specs=in_specs, out_specs=out_specs, out_shape=out_shape,
        scratch_shapes=list(scratch), name=name,
        compiler_params=pltpu.CompilerParams(vmem_limit_bytes=VMEM_LIMIT,
                                             dimension_semantics=('arbitrary',) * len(grid),
                                             collective_id=collective_id,
                                             has_side_effects=collective_id is not None),
        cost_estimate=pl.CostEstimate(flops=flops, bytes_accessed=moved, transcendentals=0))(*args)


def layer_compute(tokens, grad_y, vec_part, weights):
    seqs, seq_len = tokens.shape
    dim, ff = grad_y.shape[2], weights[2].shape[1]
    n_tok, pairs, half = seqs * seq_len, dim // PAIR, dim // 2
    cos, sin = rope_tables(seq_len)
    tok_seq = tokens.reshape(seqs, 1, seq_len)
    any_spec = pl.BlockSpec(memory_space=pl.ANY)
    wide = shape_of((n_tok, dim), BF16)
    wide_f32 = shape_of((n_tok, dim), F32)

    def rows_spec(rows, width=dim):
        return pl.BlockSpec((rows, width), lambda i: (i, 0))

    def wholes(*arrays):
        return [whole(a.shape) for a in arrays]

    def sems(*counts):
        return [pltpu.SemaphoreType.DMA((n,)) for n in counts]

    tile = 256
    per_seq = seq_len // tile
    table_spec = pl.BlockSpec((tile, PAIR), lambda i: (i % per_seq, 0))
    full = [shape_of((2 * w.shape[0],) + w.shape[1:], BF16) for w in weights]
    vec_shape = shape_of((2,) + vec_part.shape, BF16)
    x_in, q, k, v, vec, w_qkv, w_out, w_fc1, w_fc2 = call(
        qkv_kernel, (n_tok // tile,),
        [pl.BlockSpec((1, 1, seq_len), lambda i: (i // per_seq, 0, 0)),
         pl.BlockSpec((1, 1, tile), lambda i: (i, 0, 0)), any_spec, table_spec, table_spec] + [any_spec] * 4,
        [rows_spec(tile)] * 4 + wholes(vec_shape) + [any_spec] * 4, [wide] * 4 + [vec_shape] + full,
        (tok_seq, tokens.reshape(n_tok // tile, 1, tile), vec_part, cos, sin) + tuple(weights),
        6 * n_tok * dim * dim,
        scratch=[pltpu.VMEM(full[0].shape, BF16), pltpu.VMEM(vec_shape.shape, BF16)]
        + [pltpu.VMEM(w.shape, BF16) for w in weights[1:]] + sems(5, 5, 9), name='qkv', collective_id=2)

    head_spec = pl.BlockSpec((seq_len, PAIR), lambda b, p: (b, p))
    tok_spec = pl.BlockSpec((1, 1, seq_len), lambda b, p: (b, 0, 0))
    lse_spec = pl.BlockSpec((1, 2, seq_len), lambda b, p: (b * pairs + p, 0, 0))
    ctx, lse = call(
        attn_fwd_kernel, (seqs, pairs), [head_spec] * 3 + [tok_spec], [head_spec, lse_spec],
        [wide, shape_of((seqs * pairs, 2, seq_len), F32)],
        (q, k, v, tok_seq), 16 * n_tok * seq_len * dim, name='attn_fwd')

    tile = 512
    pages = shape_of((ff // dim, dim, dim), F32)
    grads = [shape_of(w_out.shape, F32), pages, shape_of(w_fc2.shape, F32), shape_of((8, dim), F32),
             shape_of((1, ff), F32)]
    hidden, d_mid, d_ctx, gw_out, gw_fc1, gw_fc2, small_two, g_b1 = call(
        ffn_kernel, (n_tok // tile,), [rows_spec(tile)] * 3 + wholes(w_out, w_fc1, w_fc2, vec),
        [rows_spec(tile)] * 3 + wholes(*grads), [wide, wide_f32, wide] + grads,
        (ctx, x_in, grad_y.reshape(n_tok, dim), w_out, w_fc1, w_fc2, vec),
        6 * n_tok * dim * (dim + 2 * ff), scratch=[pltpu.VMEM((tile, dim), F32)] * 2, name='ffn')

    blocks = (3, RING, RING, half // (3 * RING * RING), dim)
    whole_table = pl.BlockSpec((seq_len, PAIR), lambda b, p: (0, 0))
    red_shape = shape_of((3, 2) + blocks[3:], F32)
    sum_shape = shape_of((seqs * pairs, 3, PAIR), F32)
    n_sems = 2 + 6 * FLOW_SEMS
    dq, dk, dv, b_sums, red = call(
        attn_bwd_reduce_kernel, (seqs, pairs),
        [head_spec] * 4 + [lse_spec, tok_spec, whole_table, whole_table, any_spec, any_spec],
        [head_spec] * 3 + [pl.BlockSpec((1, 3, PAIR), lambda b, p: (b * pairs + p, 0, 0))] + wholes(red_shape),
        [wide] * 3 + [sum_shape, red_shape],
        (q, k, v, d_ctx, lse, tok_seq, cos, sin, gw_fc2.reshape((2, RING) + blocks), gw_fc1.reshape((RING, 2) + blocks)),
        40 * n_tok * seq_len * dim,
        scratch=[pltpu.VMEM((seq_len, PAIR), F32)] * 2 + [pltpu.VMEM((RING, 2) + blocks, F32)] * 2
        + comm_temps(2, blocks[3], dim) + sems(n_sems, n_sems, 2), name='attn_bwd', collective_id=0)

    n_sems = 16 + 12 * FLOW_SEMS
    fc2, fc1, out, qkv, small_sum = call(
        qkv_bwd_reduce_kernel, (seqs,),
        [pl.BlockSpec((1, 1, seq_len), lambda i: (i, 0, 0))] + [rows_spec(seq_len)] * 5
        + wholes(w_qkv, vec, red, small_two, g_b1, b_sums) + [any_spec],
        [any_spec] * 4 + [whole((SMALL_ROWS, half))],
        [shape_of((RING,) + blocks, F32), shape_of(blocks[:-1] + (ff,), F32), shape_of(blocks, F32),
         shape_of(blocks[:-1] + (3 * dim,), F32), shape_of((SMALL_ROWS, half), F32)],
        (tok_seq, x_in, dq, dk, dv, d_mid, w_qkv, vec, red, small_two, g_b1, b_sums, gw_out.reshape((2,) + blocks)),
        12 * n_tok * dim * dim,
        scratch=[pltpu.VMEM((RING, 2) + blocks, F32), pltpu.VMEM((RING, 1) + blocks, F32)]
        + comm_temps(1, blocks[3], dim)
        + [pltpu.VMEM((RING, 2) + blocks, F32), pltpu.VMEM((2, SMALL_ROWS, half), F32),
           pltpu.VMEM((SMALL_ROWS, half), F32), pltpu.VMEM((3, RING, SMALL_ROWS, half), F32)]
        + sems(n_sems, n_sems, 10), name='qkv_bwd', collective_id=1)
    big = (qkv.reshape(half, 3 * dim), out.reshape(half, dim), fc1.reshape(half, ff), fc2.reshape(ff // 2, dim))
    return hidden.reshape(grad_y.shape), big, small_sum


RING = 4
ALL = slice(None)
ORDERS = ('xyz', 'yzx', 'zxy')
STRIDE = {'x': 1, 'y': RING, 'z': RING * RING}
MESH_ID = pl.DeviceIdType.MESH


class Torus:
    def __init__(self):
        self.me = lax.axis_index('dp')
        self.part = lax.axis_index('fsdp')
        self.coord = {axis: self.me // stride % RING for axis, stride in STRIDE.items()}

    def at(self, axis, delta):
        return (self.coord[axis] + delta + RING) % RING

    def chip(self, axis, delta):
        return {'dp': self.me + (self.at(axis, delta) - self.coord[axis]) * STRIDE[axis]}

    def partner(self):
        return {'fsdp': 1 - self.part}

    def greet(self):
        barrier = pltpu.get_barrier_semaphore()
        peers = [self.partner()] + [self.chip(axis, delta) for axis in 'xyz' for delta in (1, -1)]
        for peer in peers:
            pl.semaphore_signal(barrier, inc=1, device_id=peer, device_id_type=MESH_ID)
        pl.semaphore_wait(barrier, len(peers))


class Flow:
    def __init__(self, torus, order, sign, view, temp_view, grads, sums, temps, sends, recvs, base):
        self.torus, self.order, self.sign = torus, order, sign
        self.view, self.temp_view = view, temp_view
        self.grads, self.sums, self.temps = grads, sums, temps
        self.sends, self.recvs, self.base = sends, recvs, base
        self.used = []

    def route(self, slot):
        level, kind = slot % 9 // 3, slot % 3
        sign = self.sign
        if slot < 9:
            target = self.temp_view(self.temps, level, kind)
            if kind == 2:
                return self.temp_view(self.temps, level, 0), target, level, sign
            delta = (2, -sign)[kind]
            return self.view(self.grads, self.place(level, delta)), target, level, (sign, -sign)[kind]
        if kind == 2:
            block = self.view(self.sums, self.place(level, -sign))
            return block, block, level, sign
        target = self.view(self.sums, self.place(level + 1))
        source = self.final(self) if level == 2 else target
        return source, target, level, (sign, -sign)[kind]

    def copy(self, slot):
        src, dst, level, delta = self.route(slot)
        return pltpu.make_async_remote_copy(
            src_ref=src, dst_ref=dst, send_sem=self.sends.at[self.base + slot],
            recv_sem=self.recvs.at[self.base + slot],
            device_id=self.torus.chip(self.order[level], delta), device_id_type=MESH_ID)

    def start(self, slot):
        self.used.append(slot)
        self.copy(slot).start()

    def wait(self, slot):
        self.copy(slot).wait_recv()

    def place(self, level, delta=None):
        own = [self.torus.coord[axis] for axis in self.order[:level]]
        return tuple(own) + (() if delta is None else (self.torus.at(self.order[level], delta),))

    def scatter_start(self, level):
        self.start(level * 3)
        self.start(level * 3 + 1)

    def scatter_mid(self, level):
        self.wait(level * 3)
        relay = self.temp_view(self.temps, level, 0)
        relay[...] = relay[...] + self.view(self.grads, self.place(level, self.sign))[...]
        self.start(level * 3 + 2)

    def scatter_end(self, level):
        self.wait(level * 3 + 1)
        self.wait(level * 3 + 2)
        mine = self.view(self.grads, self.place(level, 0))
        mine[...] = mine[...] + self.temp_view(self.temps, level, 1)[...] + self.temp_view(self.temps, level, 2)[...]

    def gather_start(self, level):
        if level == 2:
            self.view(self.sums, self.place(3))[...] = self.final(self)[...]
        self.start(9 + level * 3)
        self.start(10 + level * 3)

    def gather_mid(self, level):
        self.wait(9 + level * 3)
        self.start(11 + level * 3)

    def gather_end(self, level):
        self.wait(10 + level * 3)
        self.wait(11 + level * 3)

    def scatter_next(self, level):
        self.scatter_end(level)
        if level == 2:
            self.gather_start(level)
        else:
            self.scatter_start(level + 1)

    def gather_next(self, level):
        self.gather_end(level)
        self.gather_start(level - 1)

    def finish(self):
        for slot in self.used:
            self.copy(slot).wait_send()


FLOW_SEMS = 18


def own_block(flow):
    return flow.view(flow.grads, flow.place(3))


def make_flows(torus, width, grads, sums, temps, sends, recvs, base, group=ALL, final=own_block):
    half = width // 2
    flows = []
    for color, order in enumerate(ORDERS):
        for side, sign in enumerate((1, -1)):
            lanes = pl.ds(side * half, half)

            def view(ref, place, color=color, lanes=lanes):
                rest = place[1:] + (ALL,) * (4 - len(place))
                return ref.at[(place[0], group if ref is grads else ALL, color) + rest + (lanes,)]

            def temp_view(refs, level, kind, color=color, lanes=lanes):
                return refs[level].at[(kind, ALL, color) + (ALL,) * (3 - level) + (lanes,)]

            flow = Flow(torus, order, sign, view, temp_view, grads, sums, temps, sends, recvs,
                        base + len(flows) * FLOW_SEMS)
            flow.final, flow.color, flow.lanes = final, color, lanes
            flows.append(flow)
    return flows


def each(flows, name, level):
    for flow in flows:
        getattr(flow, name)(level)


def comm_temps(groups, rows, dim):
    return [pltpu.VMEM((3, groups, 3) + (RING,) * (2 - level) + (rows, dim), F32) for level in range(3)]


def attn_bwd_reduce_kernel(q, k, v, d_ctx, lse, tok_seq, cos, sin, fc2, fc1, dq_out, dk_out, dv_out, sums_out, red,
                           dk_acc, dv_acc, grads, other_sum, temp0, temp1, temp2, sends, recvs, local):
    torus = Torus()
    step = pl.program_id(0) * pl.num_programs(1) + pl.program_id(1)
    flows = make_flows(torus, grads.shape[-1], grads, None, (temp0, temp1, temp2), sends, recvs, 2)
    sources = (lambda i: fc2.at[i], lambda i: fc1.at[:, i])

    def remote(n):
        return pltpu.make_async_remote_copy(
            src_ref=sources[n](1 - torus.part), dst_ref=other_sum.at[:, n], send_sem=sends.at[n], recv_sem=recvs.at[n],
            device_id=torus.partner(), device_id_type=MESH_ID)

    def mine(n):
        return pltpu.make_async_copy(sources[n](torus.part), grads.at[:, n], local.at[n])

    @pl.when(step == 0)
    def _():
        torus.greet()
        for n in range(2):
            remote(n).start()
            mine(n).start()

    @pl.when(step == 4)
    def _():
        for n in range(2):
            remote(n).wait_recv()
            mine(n).wait()

            @pl.loop(0, RING * 3)
            def _(i):
                grads[i // 3, n, i % 3] = grads[i // 3, n, i % 3] + other_sum[i // 3, n, i % 3]
        each(flows, 'scatter_start', 0)

    @pl.when(step == 8)
    def _():
        each(flows, 'scatter_mid', 0)

    @pl.when(step == 10)
    def _():
        each(flows, 'scatter_next', 0)

    @pl.when(step == 11)
    def _():
        each(flows, 'scatter_mid', 1)

    attn_bwd_kernel(q, k, v, d_ctx, lse, tok_seq, cos, sin, dq_out, dk_out, dv_out, sums_out, dk_acc, dv_acc)

    @pl.when(step == 11)
    def _():
        each(flows, 'scatter_next', 1)
        each(flows, 'scatter_mid', 2)
        each(flows, 'scatter_end', 2)
        for flow in flows:
            red[flow.color, :, :, flow.lanes] = own_block(flow)[...]
        for n in range(2):
            remote(n).wait_send()
        for flow in flows:
            flow.finish()


def qkv_bwd_reduce_kernel(tok_seq, x_in, dq, dk, dv, d_mid, w_qkv, vec, red, small_two, g_b1, b_sums,
                          gw_out, fc2_sum, fc1_sum, out_sum, qkv_sum, small_sum,
                          grads, sums, temp0, temp1, temp2, sums_ab, small, small_other, small_slots,
                          sends, recvs, local):
    torus = Torus()
    step = pl.program_id(0)
    last = pl.num_programs(0) - 1
    dim = x_in.shape[1]
    half = dim // 2
    part = torus.part

    def final(flow):
        return red.at[flow.color, :, :, flow.lanes]

    gathers = make_flows(torus, dim, None, sums_ab, None, sends, recvs, 16, final=final)
    flows = make_flows(torus, dim, grads, sums, (temp0, temp1, temp2), sends, recvs, 16 + 6 * FLOW_SEMS,
                       group=pl.ds(part, 1))

    def load_out():
        return pltpu.make_async_copy(gw_out, grads.at[0], local.at[0])

    def later_hook():
        each(gathers, 'gather_next', 2)
        each(gathers, 'gather_mid', 1)

    hooks = ((0, 1, lambda: each(gathers, 'gather_mid', 2)), (0, 2, later_hook), (1, 0, lambda: each(gathers, 'gather_next', 1)))

    @pl.when(step == 0)
    def _():
        torus.greet()
        load_out().start()
        each(gathers, 'gather_start', 2)
        small[...] = jnp.zeros_like(small)
        for page in range(1, RING):
            grads[page] = jnp.zeros(grads.shape[1:], F32)

    x_hat, inv_std = hat_of(x_in[...].astype(F32))
    gain = vec_row(vec, 'ln1_gain')
    h_one = (x_hat * gain + vec_row(vec, 'ln1_bias')).astype(BF16)
    d_one = None
    for index, ref in enumerate((dq, dk, dv)):
        for at_step, at_index, hook in hooks:
            if at_index == index:
                pl.when(step == at_step)(hook)
        cols = slice(index * dim, (index + 1) * dim)
        d_part = ref[...]
        grads[index + 1] += dot(h_one, d_part, TN).reshape(grads.shape[1:])
        new = dot(d_part, w_qkv[:, cols], NT)
        d_one = new if index == 0 else d_one + new
    g_rows = jnp.concatenate([col_sum(d_one * x_hat), col_sum(d_one)], axis=0)
    d_in = d_mid[...] + hat_bwd(d_one, x_hat, inv_std, gain)
    scale, _ = seq_counts(tok_seq[0])
    one_hot = live_one_hot(tok_seq[0], EMB_ROWS)
    high = d_in.astype(BF16)
    low = (d_in - high.astype(F32)).astype(BF16)
    g_emb = (dot(one_hot, high) + dot(one_hot, low)) * scale
    for side in range(2):
        lanes = slice(side * half, (side + 1) * half)
        small[side, :EMB_ROWS, :] += g_emb[:, lanes]
        small[side, EMB_ROWS:EMB_ROWS + 2, :] += g_rows[:, lanes]

    @pl.when(step == last)
    def _():
        load_out().wait()
        pairs = dim // 128
        per_pair = [b_sums[p] for p in range(pairs)]
        for b in range(1, b_sums.shape[0] // pairs):
            per_pair = [per_pair[p] + b_sums[b * pairs + p] for p in range(pairs)]
        b_qkv = jnp.concatenate([per_pair[p][i:i + 1] for i in range(3) for p in range(pairs)], axis=1)
        for side in range(2):
            row = EMB_ROWS + 2
            small[side, row:row + 4, :] = small_two[:4, side * half:(side + 1) * half]
            row += 4
            for grad in (b_qkv, g_b1[...]):
                base = side * (grad.shape[1] // 2)
                for i in range(grad.shape[1] // dim):
                    small[side, row:row + 1, :] = grad[:, base + i * half:base + (i + 1) * half]
                    row += 1
        pair_copies = [
            pltpu.make_async_remote_copy(
                src_ref=small.at[1 - part], dst_ref=small_other, send_sem=sends.at[0], recv_sem=recvs.at[0],
                device_id=torus.partner(), device_id_type=MESH_ID)] + [
            pltpu.make_async_remote_copy(
                src_ref=grads.at[page, 1 - part], dst_ref=sums.at[page, 0], send_sem=sends.at[1 + page],
                recv_sem=recvs.at[1 + page], device_id=torus.partner(), device_id_type=MESH_ID)
            for page in range(RING)]
        for copy in pair_copies:
            copy.start()
        started = list(pair_copies)

        def small_start(level, value):
            axis = ORDERS[0][level]
            here = torus.coord[axis]
            small_slots[level, here] = value
            slot = small_slots.at[level, here]
            copies = [pltpu.make_async_remote_copy(
                src_ref=slot, dst_ref=slot, send_sem=sends.at[5 + level * 3 + n], recv_sem=recvs.at[5 + level * 3 + n],
                device_id=torus.chip(axis, delta), device_id_type=MESH_ID) for n, delta in enumerate((1, -1, 2))]
            for copy in copies:
                copy.start()
            started.extend(copies)
            return copies

        def small_end(level, copies):
            for copy in copies:
                copy.wait_recv()
            return ((small_slots[level, 0] + small_slots[level, 1]) + small_slots[level, 2]) + small_slots[level, 3]

        pair_copies[0].wait_recv()
        small_copies = small_start(0, small[part] + small_other[...])
        for page in range(RING):
            pair_copies[1 + page].wait_recv()

            @pl.loop(0, 3)
            def _(i):
                grads[page, part, i] = grads[page, part, i] + sums[page, 0, i]
        each(flows, 'scatter_start', 0)
        each(gathers, 'gather_mid', 0)
        for level in range(3):
            each(flows, 'scatter_mid', level)
            total = small_end(level, small_copies)
            if level < 2:
                small_copies = small_start(level + 1, total)
            each(flows, 'scatter_next', level)
        small_sum[...] = total
        each(gathers, 'gather_end', 0)
        stores = [pltpu.make_async_copy(sums_ab.at[:, 0], fc2_sum, local.at[1])]
        for page in range(RING):
            lanes = pl.ds(page * dim, dim)
            stores.append(pltpu.make_async_copy(sums_ab.at[page, 1], fc1_sum.at[:, :, :, :, lanes], local.at[2 + page]))
        for store in stores:
            store.start()
        each(flows, 'gather_mid', 2)
        for level in (1, 0):
            each(flows, 'gather_next', level + 1)
            each(flows, 'gather_mid', level)
        each(flows, 'gather_end', 0)
        tail = [pltpu.make_async_copy(sums.at[0, 0], out_sum, local.at[6])]
        for page in range(3):
            tail.append(pltpu.make_async_copy(
                sums.at[page + 1, 0], qkv_sum.at[:, :, :, :, pl.ds(page * dim, dim)], local.at[7 + page]))
        for store in tail:
            store.start()
        for copy in started:
            copy.wait_send()
        for flow in gathers + flows:
            flow.finish()
        for store in stores + tail:
            store.wait()


def solution(mesh):
    row_spec = P(('dp', 'fsdp'), None)
    act_spec = P(('dp', 'fsdp'), None, None)
    param_specs = (P(None, 'fsdp'),) + (P('fsdp'),) * 12

    def local_step(tokens, grad_y, *shards):
        (embedding, ln1_gain, ln1_bias, w_qkv, b_qkv, w_out, b_out,
         ln2_gain, ln2_bias, w_fc1, b_fc1, w_fc2, b_fc2) = shards
        vectors = (ln1_gain, ln1_bias, b_out, ln2_gain, ln2_bias, b_fc2, b_qkv, b_fc1)
        vocab, width = embedding.shape
        rows = [vec.reshape(-1, width) for vec in vectors]
        vec_part = jnp.concatenate([jnp.pad(embedding, ((0, VEC_ROW - vocab), (0, 0)))] + rows)
        vec_part = jnp.pad(vec_part, ((0, SMALL_ROWS - vec_part.shape[0]), (0, 0)))
        hidden, big, small_sum = layer_compute(tokens, grad_y, vec_part, (w_qkv, w_out, w_fc1, w_fc2))
        g_w_qkv, g_w_out, g_w_fc1, g_w_fc2 = big
        g_embedding = small_sum[:vocab]
        start = EMB_ROWS
        vec_grads = []
        for row in rows:
            vec_grads.append(small_sum[start:start + row.shape[0]].reshape(-1))
            start += row.shape[0]
        (g_ln1_gain, g_ln1_bias, g_b_out, g_ln2_gain, g_ln2_bias, g_b_fc2, g_b_qkv, g_b_fc1) = vec_grads
        return (hidden, g_embedding, g_ln1_gain, g_ln1_bias, g_w_qkv, g_b_qkv, g_w_out, g_b_out,
                g_ln2_gain, g_ln2_bias, g_w_fc1, g_b_fc1, g_w_fc2, g_b_fc2)

    return jax.shard_map(local_step, mesh=mesh, in_specs=(row_spec, act_spec) + param_specs,
                         out_specs=(act_spec,) + param_specs, check_vma=False)
```

time: 897 us -> 373 us (0.42)
  waiting for transfers between devices: 355 us -> 0 us
  Pallas kernels: 0 us -> 340 us
  matrix products: 295 us -> 0 us
  other arithmetic: 126 us -> 0.01 us
  local copies, waits for them, and re-layouts: 80.1 us -> 26.4 us
  blocking collectives: 20 us -> 0 us
  between operations: 16.9 us -> 0.89 us
    pallas_call x0 -> x5, Pallas kernels: none -> 340 us  [call(): pl.pallas_call(kernel, grid=grid, in_specs=in_specs, out_specs=out_specs,...]
    psum x2 -> x0, waiting for transfers between devices: 323 us -> none  [the longest x1 200 us: local_step(): lax.psum(lax.psum_scatter(full_grad, 'fsdp', scatter_dimension=0, tiled=T...]
    dot_general x19 -> x0, matrix products: 269 us -> none  [f32_einsum(): return jnp.einsum(form, lhs, rhs, preferred_element_type=jnp.float32)]
    convert_element_type x11 -> x0, other arithmetic: 93.5 us -> none  [the longest x1 47.1 us: layer_step(): act_b16 = hidden_act.astype(jnp.bfloat16)]
    unnamed x177 -> x14, local copies, waits for them, and re-layouts: 43.2 us -> 10.9 us
    reduce_scatter x5 -> x0, waiting for transfers between devices: 30 us -> none  [the longest x4 30 us: local_step(): lax.psum_scatter(full_grad, 'fsdp', scatter_dimension=0, tiled=True)]
    sub x1 -> x0, matrix products: 26.2 us -> none  [layer_step(): attn_prob = jax.nn.softmax(scores, axis=-1)]
    reduce_sum x7 -> x0, other arithmetic: 20 us -> none  [the longest x2 9.61 us: norm_bwd(): jnp.sum(d_out * x_hat, axis=(0, 1))]
  transfers between devices with their start and end apart: 11 -> 0, of which waited for: 4 -> 0; matrix products, arithmetic and copies ran while one was open for 28% -> 0% of each run, Pallas kernels for 0% -> 0%
where the time goes in v1:
time: 373 us; the launch traced here: 368 us
  Pallas kernels  340 us (91%)
  local copies, waits for them, and re-layouts  26.4 us (7%)
    pallas_call x5, Pallas kernels, call(): pl.pallas_call(kernel, grid=grid, in_specs=in_specs, out_specs=out_specs,...  340 us
    unnamed x14, local copies, waits for them, and re-layouts  10.9 us

profile of v1, /device:TPU:0, one launch (start us, length us, event | category | flops | bytes accessed | tf_op | source)
XLA Modules:
  0.0 367.6 jit_solution(4153751142206603153)
XLA Ops:
  0.6 0.7 reshape.111
  1.3 0.7 reshape.112
  2.0 0.7 reshape.113
  2.7 0.7 reshape.114
  3.4 0.7 reshape.115
  4.1 0.7 reshape.116
  4.7 0.7 reshape.117
  5.4 0.7 reshape.118
  6.1 1.3 reshape.109.tok_seq
  7.4 1.3 reshape.110.tok_tile
  8.7 0.8 pad.8
  9.5 0.2 concatenate.3
  9.7 0.6 pad.9.vec_part
  10.3 16.4 %qkv.1 = (bf16[1536,768]{1,0:T(8,128)(2,1)}, bf16[1536,768]{1,0:T(8,128)(2,1)}, bf16[1536,768]{1,0:T(8,128)(2,1)}, bf16[1536,768]{1,0:T(8,128)(2,1)}, bf16[2,64,...) custom-call(s32[2,1,768]{2,1,0:T(1,128)} %reshape.109.tok_seq, ...), custom_call_target="tpu_custom_call" | custom-call | flops 5435817984 | bytes 31617024 | tf_op jit(solution)/shard_map/qkv/pallas_call | solution.py:301
  26.7 50.0 %attn_fwd.1 = (bf16[1536,768]{1,0:T(8,128)(2,1)}, f32[12,2,768]{2,1,0:T(2,128)}) custom-call(bf16[1536,768]{1,0:T(8,128)(2,1)} %get-tuple-element.43.q, bf16[1536,768]{1,0:T(8,128)(2,1)} %get-tuple-element.44.k, bf16[1536,768]{1,0:T(8,128)(2,1)} %get-tuple-element.45.v, s32[2,1,768]{2,1,0:T(1,128)} %reshape.109.tok_seq), custom_call_target="tpu_custom_call" | custom-call | flops 14495514624 | bytes 9517056 | tf_op jit(solution)/shard_map/attn_fwd/pallas_call | solution.py:301
  76.7 81.4 %ffn.1 = (bf16[1536,768]{1,0:T(8,128)(2,1)}, f32[1536,768]{1,0:T(8,128)}, bf16[1536,768]{1,0:T(8,128)(2,1)}, f32[768,768]{1,0:T(8,128)}, f32[4,768,768]{2,1,0:T(...) custom-call(bf16[1536,768]{1,0:T(8,128)(2,1)} %get-tuple-element.46.ctx, ...), custom_call_target="tpu_custom_call" | custom-call | flops 48922361856 | bytes 48500736 | tf_op jit(solution)/shard_map/ffn/pallas_call | solution.py:301
  158.1 76.8 %attn_bwd.1 = (bf16[1536,768]{1,0:T(8,128)(2,1)}, bf16[1536,768]{1,0:T(8,128)(2,1)}, bf16[1536,768]{1,0:T(8,128)(2,1)}, f32[12,3,128]{2,1,0:T(4,128)}, f32[3,2,8,768]{3,2,1,0:T(8,128)}) custom-call(bf16[1536,768]{1,0:T(8,128)(2,1)} %get-tuple-element.43.q, bf16[1536,768]{1,0:T(8,128)(2,1)} %get-tuple-element.44.k, bf16[1536,768]{1,0:T(8,128)(2,1)} %get-tuple-element.45.v, ...), custom_call_target="tpu_custom_call" | custom-call | flops 36238786560 | bytes 36421632 | tf_op jit(solution)/shard_map/attn_bwd/pallas_call | solution.py:301
  234.9 115.8 %qkv_bwd.1 = (f32[4,3,4,4,8,768]{5,4,3,2,1,0:T(8,128)}, f32[3,4,4,8,3072]{4,3,2,1,0:T(8,128)}, f32[3,4,4,8,768]{4,3,2,1,0:T(8,128)}, f32[3,4,4,8,2304]{4,3,2,1,0:T(8,128)}, f32[64,384]{1,0:T(8,128)}) custom-call(s32[2,1,768]{2,1,0:T(1,128)} %reshape.109.tok_seq, bf16[1536,768]{1,0:T(8,128)(2,1)} %get-tuple-element.47.x_in, ...), custom_call_target="tpu_custom_call" | custom-call | flops 10871635968 | bytes 34615296 | tf_op jit(solution)/shard_map/qkv_bwd/pallas_call | solution.py:301
  350.7 0.7 slice.30
  351.4 0.6 reshape.127
  352.0 0.7 slice.34
  352.8 0.6 reshape.133
  353.4 1.6 slice_reduce_fusion
  354.9 1.6 slice.27
  356.5 4.1 %copy.35 = f32[384,2304]{1,0:T(8,128)} copy(f32[384,2304]{1,0:T(8,128)} %bitcast.15) | data formatting | bytes 7077888
  360.7 0.0 copy-done
  360.7 1.0 copy.36
  361.7 0.0 slice-done.2
  361.7 2.4 copy.37
  364.1 0.8 slice-done
  364.9 0.3 slice-done.1
  365.3 2.2 copy.38
  (8 shorter events, 0.0 us)
Async XLA Ops:
  354.9 6.8 %slice-start.2 = ((s8[4718592]{0:T(1024)(128)(4,1)}), s8[4194304]{0:T(1024)(128)(4,1)S(1)}, s32[]{:S(2)}) async-start(s8[4718592]{0:T(1024)(128)(4,1)} %bitcast.12), calls=%async_computation.2 | async-start | bytes 8388608
  356.5 4.2 %copy-start = (f32[3,4,4,8,768]{4,3,2,1,0:T(8,128)S(1)}, f32[3,4,4,8,768]{4,3,2,1,0:T(8,128)}, u32[]{:S(2)}) copy-start(f32[3,4,4,8,768]{4,3,2,1,0:T(8,128)} %get-tuple-element.69) | copy-start | bytes 3538948
  356.5 5.2 %slice-start.3 = ((s8[4718592]{0:T(1024)(128)(4,1)}), s8[524288]{0:T(1024)(128)(4,1)S(1)}, s32[]{:S(2)}) async-start(s8[4718592]{0:T(1024)(128)(4,1)} %bitcast.12), calls=%async_computation.3 | async-start | bytes 1048576
  360.7 4.2 %slice-start = ((s8[4718592]{0:T(1024)(128)(4,1)}), s8[4194304]{0:T(1024)(128)(4,1)S(1)}, s32[]{:S(2)}) async-start(s8[4718592]{0:T(1024)(128)(4,1)} %bitcast.9), calls=%async_computation | async-start | bytes 8388608
  361.7 3.5 slice-start.1

commit v2 on v1

--- a/solution.py
+++ b/solution.py
@@ -19,6 +19,7 @@
 SMALL_ROWS = 64
 VEC_ROW = 48
 VECTORS = ('ln1_gain', 'ln1_bias', 'b_out', 'ln2_gain', 'ln2_bias', 'b_fc2', 'b_qkv', 'b_fc1')
+SCALE = HEAD_DIM ** -0.5
 VMEM_LIMIT = 60 << 20
 
 NN = (((1,), (0,)), ((), ()))
@@ -95,7 +96,7 @@
     return jnp.where((iota(x_val.shape, 1) >= HEAD_DIM) == (head == 1), x_val, jnp.zeros_like(x_val))
 
 
-def qkv_kernel(tok_seq, tok_tile, vec_part, cos, sin, wq_part, wo_part, w1_part, w2_part,
+def qkv_kernel(tok_seq, vec_part, cos, sin, wq_part, wo_part, w1_part, w2_part,
                x_out, q_out, k_out, v_out, vec_out, wq_out, wo_out, w1_out, w2_out,
                w_qkv, vec, wo_own, w1_own, w2_own, sends, recvs, local):
     step = pl.program_id(0)
@@ -146,9 +147,12 @@
         store_qkv().start()
         vec_out[...] = vec[...]
 
+    per_seq = tok_seq.shape[2] // x_out.shape[0]
+    first = lax.rem(step, per_seq) * x_out.shape[0]
+    tok_tile = tok_seq[0, :, pl.ds(pl.multiple_of(first, x_out.shape[0]), x_out.shape[0])]
     scale, _ = seq_counts(tok_seq[0])
     emb = jnp.concatenate([vec[side, :VEC_ROW, :] for side in range(2)], axis=1)
-    x_b16 = (dot(live_one_hot(tok_tile[0], VEC_ROW), emb, TN) * scale).astype(BF16)
+    x_b16 = (dot(live_one_hot(tok_tile, VEC_ROW), emb, TN) * scale).astype(BF16)
     x_out[...] = x_b16
     x_hat, _ = hat_of(x_b16.astype(F32))
     h_one = (x_hat * vec_row(vec, 'ln1_gain') + vec_row(vec, 'ln1_bias')).astype(BF16)
@@ -161,7 +165,7 @@
             out[...] = proj.astype(BF16)
             continue
         if out is q_out:
-            proj = proj * HEAD_DIM ** -0.5
+            proj = proj * SCALE
         for first in range(0, dim, PAIR):
             pair = slice(first, first + PAIR)
             z = proj[:, pair]
@@ -178,104 +182,126 @@
 
 
 PAIR = 2 * HEAD_DIM
-CHUNK = 256
-
-
-def pad_bias(tok_row, keys):
+def pad_bias(tok_row):
     _, real = seq_counts(tok_row)
-    return jnp.where(iota((keys, CHUNK), 0).astype(F32) < real, 0.0, -1e30)
+    size = tok_row.shape[1]
+    return jnp.where(iota((size, size), 0).astype(F32) < real, 0.0, -1e30)
+
+
+def head_rows(head):
+    return slice(head * HEAD_DIM, (head + 1) * HEAD_DIM)
 
 
 def attn_fwd_kernel(q, k, v, tok_seq, ctx, lse):
-    q_t = q[...].T
-    v_t = v[...].T
-    k_val = k[...]
-    pad_tab = pad_bias(tok_seq[0], q.shape[0])
-    for c in range(q.shape[0] // CHUNK):
-        cols = slice(c * CHUNK, (c + 1) * CHUNK)
-        parts = []
-        for head in range(2):
-            s_t = dot(k_val, rows_of_head(q_t[:, cols], head)) + pad_tab
-            top = jnp.max(s_t, axis=0, keepdims=True)
-            e_t = jnp.exp(s_t - top)
-            total = col_sum(e_t)
-            lse[0, head:head + 1, cols] = top + jnp.log(total)
-            p_t = (e_t * (1.0 / total)).astype(BF16)
-            parts.append(dot(v_t[head * HEAD_DIM:(head + 1) * HEAD_DIM, :], p_t))
-        ctx[cols, :] = jnp.concatenate(parts, axis=0).T.astype(BF16)
-
-
-def attn_bwd_kernel(q, k, v, d_ctx, lse, tok_seq, cos, sin, dq_out, dk_out, dv_out, sums, dk_acc, dv_acc):
+    q_t, v_t, k_val = q[...].T, v[...].T, k[...]
+    bias = pad_bias(tok_seq[0])
+    parts = []
+    for head in range(2):
+        s_t = dot(k_val, rows_of_head(q_t, head)) + bias
+        top = jnp.max(s_t, axis=0, keepdims=True)
+        e_t = jnp.exp(s_t - top)
+        total = col_sum(e_t)
+        lse[0, head:head + 1, :] = top + jnp.log(total)
+        p_t = (e_t * (1.0 / total)).astype(BF16)
+        parts.append(dot(v_t[head_rows(head), :], p_t))
+    ctx[...] = jnp.concatenate(parts, axis=0).T.astype(BF16)
+
+
+def attn_bwd_kernel(q, k, v, d_ctx, lse, tok_seq, cos, sin, dq_out, dk_out, dv_out, sums):
     q_val, k_val, v_val, d_val = q[...], k[...], v[...], d_ctx[...]
     q_t, k_t, d_t = q_val.T, k_val.T, d_val.T
-    pad_tab = pad_bias(tok_seq[0], q.shape[0])
-    dq_sum = jnp.zeros((1, 128), F32)
-    for c in range(q.shape[0] // CHUNK):
-        cols = slice(c * CHUNK, (c + 1) * CHUNK)
-        parts = []
-        for head in range(2):
-            s_t = dot(k_val, rows_of_head(q_t[:, cols], head)) + pad_tab
-            p_t = jnp.exp(s_t - lse[0, head:head + 1, cols])
-            dp_t = dot(v_val, rows_of_head(d_t[:, cols], head))
-            delta = col_sum(p_t * dp_t)
-            ds_t = (p_t * (dp_t - delta)).astype(BF16)
-            dv_new = dot(p_t.astype(BF16), lanes_of_head(d_val[cols, :], head))
-            dk_new = dot(ds_t, lanes_of_head(q_val[cols, :], head))
-            if c == 0 and head == 0:
-                dv_acc[...] = dv_new
-                dk_acc[...] = dk_new
-            else:
-                dv_acc[...] += dv_new
-                dk_acc[...] += dk_new
-            parts.append(dot(k_t[head * HEAD_DIM:(head + 1) * HEAD_DIM, :], ds_t))
-        z = jnp.concatenate(parts, axis=0).T
-        z = (z * cos[cols, :] - swap_halves(z) * sin[cols, :]) * HEAD_DIM ** -0.5
-        dq_sum = dq_sum + col_sum(z)
-        dq_out[cols, :] = z.astype(BF16)
-    z = dk_acc[...]
-    z = z * cos[...] - swap_halves(z) * sin[...]
-    dk_out[...] = z.astype(BF16)
-    z_v = dv_acc[...]
-    dv_out[...] = z_v.astype(BF16)
-    sums[0] = jnp.concatenate([dq_sum, col_sum(z), col_sum(z_v)], axis=0)
+    bias = pad_bias(tok_seq[0])
+    parts, d_key, d_value = [], 0.0, 0.0
+    for head in range(2):
+        s_t = dot(k_val, rows_of_head(q_t, head)) + bias
+        p_t = jnp.exp(s_t - lse[0, head:head + 1, :])
+        dp_t = dot(v_val, rows_of_head(d_t, head))
+        delta = col_sum(p_t * dp_t)
+        ds_t = (p_t * (dp_t - delta)).astype(BF16)
+        d_value += dot(p_t.astype(BF16), lanes_of_head(d_val, head))
+        d_key += dot(ds_t, lanes_of_head(q_val, head))
+        parts.append(dot(k_t[head_rows(head), :], ds_t))
+
+    def unrotate(z):
+        return z * cos[...] - swap_halves(z) * sin[...]
+
+    grads = (unrotate(jnp.concatenate(parts, axis=0).T) * SCALE, unrotate(d_key), d_value)
+    for grad, out in zip(grads, (dq_out, dk_out, dv_out)):
+        out[...] = grad.astype(BF16)
+    sums[0] = jnp.concatenate([col_sum(grad) for grad in grads], axis=0)
 
 
 FF_CHUNK = 768
 
 
-def ffn_kernel(ctx, x_in, grad_y, w_out, w_fc1, w_fc2, vec,
-               y_out, dmid_out, dctx_out, gw_out, gw_fc1, gw_fc2, g_small, g_b1, y_acc, dh_acc):
+def ffn_kernel(ctx, x_in, grad_y, wo_hbm, w1_hbm, w2_hbm, vec,
+               y_out, dmid_out, dctx_out, gwo_hbm, gw1_hbm, gw2_hbm, g_small, g_b1,
+               y_acc, dh_acc, w_out, w_fc1, w_fc2, gw_out, gw_fc1, gw_fc2, b_fc1, local):
     step = pl.program_id(0)
+    chunks = w_fc1.shape[1] // FF_CHUNK
+
+    def cols(j):
+        return pl.ds(j * FF_CHUNK, FF_CHUNK)
+
+    def loads(j):
+        if j == chunks:
+            return [pltpu.make_async_copy(wo_hbm, w_out, local.at[2 * j])]
+        return [pltpu.make_async_copy(w1_hbm.at[:, cols(j)], w_fc1.at[:, cols(j)], local.at[2 * j]),
+                pltpu.make_async_copy(w2_hbm.at[cols(j)], w_fc2.at[cols(j)], local.at[2 * j + 1])]
+
+    def stores(j):
+        if j == chunks:
+            return [pltpu.make_async_copy(gw_out, gwo_hbm, local.at[2 * j])]
+        return [pltpu.make_async_copy(gw_fc1.at[j], gw1_hbm.at[j], local.at[2 * j]),
+                pltpu.make_async_copy(gw_fc2.at[cols(j)], gw2_hbm.at[cols(j)], local.at[2 * j + 1])]
+
+    def at_first(j):
+        @pl.when(step == 0)
+        def _():
+            for copy in loads(j):
+                copy.wait()
+
+    def at_last(j):
+        @pl.when(step == pl.num_programs(0) - 1)
+        def _():
+            for copy in stores(j):
+                copy.start()
+
     @pl.when(step == 0)
     def _():
+        for j in [chunks] + list(range(chunks)):
+            for copy in loads(j):
+                copy.start()
         for ref in (gw_out, gw_fc1, gw_fc2, g_small, g_b1):
             ref[...] = jnp.zeros_like(ref)
-
-    gain, b_fc1 = vec_row(vec, 'ln2_gain'), vec_row(vec, 'b_fc1')
+        b_fc1[...] = vec_row(vec, 'b_fc1')
+
+    gain = vec_row(vec, 'ln2_gain')
     ctx_val = ctx[...]
+    at_first(chunks)
     x_mid = x_in[...].astype(F32) + dot(ctx_val, w_out[...]) + vec_row(vec, 'b_out')
     x_hat, inv_std = hat_of(x_mid)
     h_two = (x_hat * gain + vec_row(vec, 'ln2_bias')).astype(BF16)
     dy = grad_y[...]
     y_acc[...] = x_mid + vec_row(vec, 'b_fc2')
-    for j in range(w_fc1.shape[1] // FF_CHUNK):
-        cols = slice(j * FF_CHUNK, (j + 1) * FF_CHUNK)
-        pre = dot(h_two, w_fc1[:, cols]) + b_fc1[:, cols]
+    dh_acc[...] = jnp.zeros_like(dh_acc)
+    for j in range(chunks):
+        at_first(j)
+        pre = dot(h_two, w_fc1[:, cols(j)]) + b_fc1[:, cols(j)]
         cdf = 0.5 + 0.5 * lax.erf(pre * (0.5 ** 0.5))
         pdf = jnp.exp(pre * pre * -0.5) * 0.3989422804014327
         act = (pre * cdf).astype(BF16)
-        d_act = dot(dy, w_fc2[cols, :], NT)
+        d_act = dot(dy, w_fc2[cols(j), :], NT)
         d_pre = d_act * (cdf + pre * pdf)
-        y_acc[...] += dot(act, w_fc2[cols, :])
-        gw_fc2[cols, :] += dot(act, dy, TN)
-        g_b1[:, cols] += col_sum(d_pre)
+        y_acc[...] += dot(act, w_fc2[cols(j), :])
+        gw_fc2[cols(j), :] += dot(act, dy, TN)
+        g_b1[:, cols(j)] += col_sum(d_pre)
         d_pre = d_pre.astype(BF16)
         gw_fc1[j] += dot(h_two, d_pre, TN)
-        d_h = dot(d_pre, w_fc1[:, cols], NT)
-        if j == 0:
-            dh_acc[...] = d_h
-        else:
-            dh_acc[...] += d_h
+        dh_acc[...] += dot(d_pre, w_fc1[:, cols(j)], NT)
+        if j > 0:
+            at_last(j - 1)
+    at_last(chunks - 1)
     y_out[...] = y_acc[...].astype(BF16)
     d_two = dh_acc[...]
     dy_f = dy.astype(F32)
@@ -286,6 +312,13 @@
     d_mid = d_mid.astype(BF16)
     gw_out[...] += dot(ctx_val, d_mid, TN)
     dctx_out[...] = dot(d_mid, w_out[...], NT).astype(BF16)
+    at_last(chunks)
+
+    @pl.when(step == pl.num_programs(0) - 1)
+    def _():
+        for j in range(chunks + 1):
+            for copy in stores(j):
+                copy.wait()
 
 
 def whole(shape):
@@ -335,9 +368,9 @@
     x_in, q, k, v, vec, w_qkv, w_out, w_fc1, w_fc2 = call(
         qkv_kernel, (n_tok // tile,),
         [pl.BlockSpec((1, 1, seq_len), lambda i: (i // per_seq, 0, 0)),
-         pl.BlockSpec((1, 1, tile), lambda i: (i, 0, 0)), any_spec, table_spec, table_spec] + [any_spec] * 4,
+         any_spec, table_spec, table_spec] + [any_spec] * 4,
         [rows_spec(tile)] * 4 + wholes(vec_shape) + [any_spec] * 4, [wide] * 4 + [vec_shape] + full,
-        (tok_seq, tokens.reshape(n_tok // tile, 1, tile), vec_part, cos, sin) + tuple(weights),
+        (tok_seq, vec_part, cos, sin) + tuple(weights),
         6 * n_tok * dim * dim,
         scratch=[pltpu.VMEM(full[0].shape, BF16), pltpu.VMEM(vec_shape.shape, BF16)]
         + [pltpu.VMEM(w.shape, BF16) for w in weights[1:]] + sems(5, 5, 9), name='qkv', collective_id=2)
@@ -355,16 +388,17 @@
     grads = [shape_of(w_out.shape, F32), pages, shape_of(w_fc2.shape, F32), shape_of((8, dim), F32),
              shape_of((1, ff), F32)]
     hidden, d_mid, d_ctx, gw_out, gw_fc1, gw_fc2, small_two, g_b1 = call(
-        ffn_kernel, (n_tok // tile,), [rows_spec(tile)] * 3 + wholes(w_out, w_fc1, w_fc2, vec),
-        [rows_spec(tile)] * 3 + wholes(*grads), [wide, wide_f32, wide] + grads,
+        ffn_kernel, (n_tok // tile,), [rows_spec(tile)] * 3 + [any_spec] * 3 + wholes(vec),
+        [rows_spec(tile)] * 3 + [any_spec] * 3 + wholes(*grads[3:]), [wide, wide_f32, wide] + grads,
         (ctx, x_in, grad_y.reshape(n_tok, dim), w_out, w_fc1, w_fc2, vec),
-        6 * n_tok * dim * (dim + 2 * ff), scratch=[pltpu.VMEM((tile, dim), F32)] * 2, name='ffn')
+        6 * n_tok * dim * (dim + 2 * ff), scratch=[pltpu.VMEM((tile, dim), F32)] * 2 + [pltpu.VMEM(w.shape, BF16) for w in (w_out, w_fc1, w_fc2)]
+        + [pltpu.VMEM(g.shape, F32) for g in grads[:3]] + [pltpu.VMEM((1, ff), F32)] + sems(2 * ff // dim + 1), name='ffn')
 
     blocks = (3, RING, RING, half // (3 * RING * RING), dim)
     whole_table = pl.BlockSpec((seq_len, PAIR), lambda b, p: (0, 0))
     red_shape = shape_of((3, 2) + blocks[3:], F32)
     sum_shape = shape_of((seqs * pairs, 3, PAIR), F32)
-    n_sems = 2 + 6 * FLOW_SEMS
+    n_sems = 2 + 12 * SCATTER_SEMS
     dq, dk, dv, b_sums, red = call(
         attn_bwd_reduce_kernel, (seqs, pairs),
         [head_spec] * 4 + [lse_spec, tok_spec, whole_table, whole_table, any_spec, any_spec],
@@ -372,7 +406,7 @@
         [wide] * 3 + [sum_shape, red_shape],
         (q, k, v, d_ctx, lse, tok_seq, cos, sin, gw_fc2.reshape((2, RING) + blocks), gw_fc1.reshape((RING, 2) + blocks)),
         40 * n_tok * seq_len * dim,
-        scratch=[pltpu.VMEM((seq_len, PAIR), F32)] * 2 + [pltpu.VMEM((RING, 2) + blocks, F32)] * 2
+        scratch=[pltpu.VMEM((RING, 2) + blocks, F32)] * 2
         + comm_temps(2, blocks[3], dim) + sems(n_sems, n_sems, 2), name='attn_bwd', collective_id=0)
 
     n_sems = 16 + 12 * FLOW_SEMS
@@ -513,13 +547,15 @@
 
 
 FLOW_SEMS = 18
+SCATTER_SEMS = 9
 
 
 def own_block(flow):
     return flow.view(flow.grads, flow.place(3))
 
 
-def make_flows(torus, width, grads, sums, temps, sends, recvs, base, group=ALL, final=own_block):
+def make_flows(torus, width, grads, sums, temps, sends, recvs, base, group=ALL, temp_group=ALL, final=own_block,
+               spacing=FLOW_SEMS):
     half = width // 2
     flows = []
     for color, order in enumerate(ORDERS):
@@ -531,10 +567,10 @@
                 return ref.at[(place[0], group if ref is grads else ALL, color) + rest + (lanes,)]
 
             def temp_view(refs, level, kind, color=color, lanes=lanes):
-                return refs[level].at[(kind, ALL, color) + (ALL,) * (3 - level) + (lanes,)]
+                return refs[level].at[(kind, temp_group, color) + (ALL,) * (3 - level) + (lanes,)]
 
             flow = Flow(torus, order, sign, view, temp_view, grads, sums, temps, sends, recvs,
-                        base + len(flows) * FLOW_SEMS)
+                        base + len(flows) * spacing)
             flow.final, flow.color, flow.lanes = final, color, lanes
             flows.append(flow)
     return flows
@@ -549,11 +585,16 @@
     return [pltpu.VMEM((3, groups, 3) + (RING,) * (2 - level) + (rows, dim), F32) for level in range(3)]
 
 
+PLAN = ('b', '', 'e0', '', '', 'm00 e1', '', 'a00', 'm01 m10', 'a01', 'm02 a10', 'm11 a02', 'a11 m12 a12')
+
+
 def attn_bwd_reduce_kernel(q, k, v, d_ctx, lse, tok_seq, cos, sin, fc2, fc1, dq_out, dk_out, dv_out, sums_out, red,
-                           dk_acc, dv_acc, grads, other_sum, temp0, temp1, temp2, sends, recvs, local):
+                           grads, other_sum, temp0, temp1, temp2, sends, recvs, local):
     torus = Torus()
     step = pl.program_id(0) * pl.num_programs(1) + pl.program_id(1)
-    flows = make_flows(torus, grads.shape[-1], grads, None, (temp0, temp1, temp2), sends, recvs, 2)
+    sets = [make_flows(torus, grads.shape[-1], grads, None, (temp0, temp1, temp2), sends, recvs,
+                       2 + n * 6 * SCATTER_SEMS, group=pl.ds(n, 1), temp_group=pl.ds(n, 1), spacing=SCATTER_SEMS)
+            for n in range(2)]
     sources = (lambda i: fc2.at[i], lambda i: fc1.at[:, i])
 
     def remote(n):
@@ -564,49 +605,46 @@
     def mine(n):
         return pltpu.make_async_copy(sources[n](torus.part), grads.at[:, n], local.at[n])
 
-    @pl.when(step == 0)
-    def _():
+    def begin():
         torus.greet()
         for n in range(2):
             remote(n).start()
             mine(n).start()
 
-    @pl.when(step == 4)
+    def enter(n):
+        remote(n).wait_recv()
+        mine(n).wait()
+
+        @pl.loop(0, RING)
+        def _(page):
+            grads[page, n] = grads[page, n] + other_sum[page, n]
+        each(sets[n], 'scatter_start', 0)
+
+    def mid(n, level):
+        each(sets[n], 'scatter_mid', level)
+
+    def after(n, level):
+        each(sets[n], 'scatter_next' if level < 2 else 'scatter_end', level)
+
+    actions = {'b': begin, 'e': enter, 'm': mid, 'a': after}
+
+    def perform(words):
+        for word in words.split():
+            actions[word[0]](*(int(number) for number in word[1:]))
+
+    for at_step, words in enumerate(PLAN[:-1]):
+        pl.when(step == at_step)(functools.partial(perform, words))
+
+    attn_bwd_kernel(q, k, v, d_ctx, lse, tok_seq, cos, sin, dq_out, dk_out, dv_out, sums_out)
+
+    @pl.when(step == len(PLAN) - 2)
     def _():
-        for n in range(2):
-            remote(n).wait_recv()
-            mine(n).wait()
-
-            @pl.loop(0, RING * 3)
-            def _(i):
-                grads[i // 3, n, i % 3] = grads[i // 3, n, i % 3] + other_sum[i // 3, n, i % 3]
-        each(flows, 'scatter_start', 0)
-
-    @pl.when(step == 8)
-    def _():
-        each(flows, 'scatter_mid', 0)
-
-    @pl.when(step == 10)
-    def _():
-        each(flows, 'scatter_next', 0)
-
-    @pl.when(step == 11)
-    def _():
-        each(flows, 'scatter_mid', 1)
-
-    attn_bwd_kernel(q, k, v, d_ctx, lse, tok_seq, cos, sin, dq_out, dk_out, dv_out, sums_out, dk_acc, dv_acc)
-
-    @pl.when(step == 11)
-    def _():
-        each(flows, 'scatter_next', 1)
-        each(flows, 'scatter_mid', 2)
-        each(flows, 'scatter_end', 2)
-        for flow in flows:
-            red[flow.color, :, :, flow.lanes] = own_block(flow)[...]
-        for n in range(2):
+        perform(PLAN[-1])
+        for n, flows in enumerate(sets):
+            for flow in flows:
+                red[flow.color, n:n + 1, :, flow.lanes] = own_block(flow)[...]
+                flow.finish()
             remote(n).wait_send()
-        for flow in flows:
-            flow.finish()
 
 
 def qkv_bwd_reduce_kernel(tok_seq, x_in, dq, dk, dv, d_mid, w_qkv, vec, red, small_two, g_b1, b_sums,
@@ -634,7 +672,16 @@
         each(gathers, 'gather_next', 2)
         each(gathers, 'gather_mid', 1)
 
-    hooks = ((0, 1, lambda: each(gathers, 'gather_mid', 2)), (0, 2, later_hook), (1, 0, lambda: each(gathers, 'gather_next', 1)))
+    def last_hook():
+        each(gathers, 'gather_next', 1)
+        load_out().wait()
+
+    hooks = ((0, 1, lambda: each(gathers, 'gather_mid', 2)), (0, 2, later_hook), (1, 0, last_hook))
+
+    def pair_copy(page):
+        return pltpu.make_async_remote_copy(
+            src_ref=grads.at[page, 1 - part], dst_ref=sums.at[page, 0], send_sem=sends.at[1 + page],
+            recv_sem=recvs.at[1 + page], device_id=torus.partner(), device_id_type=MESH_ID)
 
     @pl.when(step == 0)
     def _():
@@ -657,6 +704,7 @@
         d_part = ref[...]
         grads[index + 1] += dot(h_one, d_part, TN).reshape(grads.shape[1:])
         new = dot(d_part, w_qkv[:, cols], NT)
+        pl.when(step == last)(pair_copy(index).start)
         d_one = new if index == 0 else d_one + new
     g_rows = jnp.concatenate([col_sum(d_one * x_hat), col_sum(d_one)], axis=0)
     d_in = d_mid[...] + hat_bwd(d_one, x_hat, inv_std, gain)
@@ -672,8 +720,8 @@
 
     @pl.when(step == last)
     def _():
-        load_out().wait()
-        pairs = dim // 128
+        pair_copy(RING - 1).start()
+        pairs = dim // PAIR
         per_pair = [b_sums[p] for p in range(pairs)]
         for b in range(1, b_sums.shape[0] // pairs):
             per_pair = [per_pair[p] + b_sums[b * pairs + p] for p in range(pairs)]
@@ -687,17 +735,11 @@
                 for i in range(grad.shape[1] // dim):
                     small[side, row:row + 1, :] = grad[:, base + i * half:base + (i + 1) * half]
                     row += 1
-        pair_copies = [
-            pltpu.make_async_remote_copy(
-                src_ref=small.at[1 - part], dst_ref=small_other, send_sem=sends.at[0], recv_sem=recvs.at[0],
-                device_id=torus.partner(), device_id_type=MESH_ID)] + [
-            pltpu.make_async_remote_copy(
-                src_ref=grads.at[page, 1 - part], dst_ref=sums.at[page, 0], send_sem=sends.at[1 + page],
-                recv_sem=recvs.at[1 + page], device_id=torus.partner(), device_id_type=MESH_ID)
-            for page in range(RING)]
-        for copy in pair_copies:
-            copy.start()
-        started = list(pair_copies)
+        small_copy = pltpu.make_async_remote_copy(
+            src_ref=small.at[1 - part], dst_ref=small_other, send_sem=sends.at[0], recv_sem=recvs.at[0],
+            device_id=torus.partner(), device_id_type=MESH_ID)
+        small_copy.start()
+        started = [small_copy] + [pair_copy(page) for page in range(RING)]
 
         def small_start(level, value):
             axis = ORDERS[0][level]
@@ -717,10 +759,10 @@
                 copy.wait_recv()
             return ((small_slots[level, 0] + small_slots[level, 1]) + small_slots[level, 2]) + small_slots[level, 3]
 
-        pair_copies[0].wait_recv()
+        small_copy.wait_recv()
         small_copies = small_start(0, small[part] + small_other[...])
         for page in range(RING):
-            pair_copies[1 + page].wait_recv()
+            started[1 + page].wait_recv()
 
             @pl.loop(0, 3)
             def _(i):
@@ -770,17 +812,18 @@
          ln2_gain, ln2_bias, w_fc1, b_fc1, w_fc2, b_fc2) = shards
         vectors = (ln1_gain, ln1_bias, b_out, ln2_gain, ln2_bias, b_fc2, b_qkv, b_fc1)
         vocab, width = embedding.shape
-        rows = [vec.reshape(-1, width) for vec in vectors]
-        vec_part = jnp.concatenate([jnp.pad(embedding, ((0, VEC_ROW - vocab), (0, 0)))] + rows)
+        flat = jnp.concatenate(vectors)
+        vec_part = jnp.concatenate([jnp.pad(embedding, ((0, VEC_ROW - vocab), (0, 0))), flat.reshape(-1, width)])
         vec_part = jnp.pad(vec_part, ((0, SMALL_ROWS - vec_part.shape[0]), (0, 0)))
         hidden, big, small_sum = layer_compute(tokens, grad_y, vec_part, (w_qkv, w_out, w_fc1, w_fc2))
         g_w_qkv, g_w_out, g_w_fc1, g_w_fc2 = big
         g_embedding = small_sum[:vocab]
         start = EMB_ROWS
         vec_grads = []
-        for row in rows:
-            vec_grads.append(small_sum[start:start + row.shape[0]].reshape(-1))
-            start += row.shape[0]
+        for vec in vectors:
+            stop = start + vec.size // width
+            vec_grads.append(small_sum[start:stop].reshape(-1))
+            start = stop
         (g_ln1_gain, g_ln1_bias, g_b_out, g_ln2_gain, g_ln2_bias, g_b_fc2, g_b_qkv, g_b_fc1) = vec_grads
         return (hidden, g_embedding, g_ln1_gain, g_ln1_bias, g_w_qkv, g_b_qkv, g_w_out, g_b_out,
                 g_ln2_gain, g_ln2_bias, g_w_fc1, g_b_fc1, g_w_fc2, g_b_fc2)

time: 373 us -> 344 us (0.922)
  Pallas kernels: 340 us -> 311 us
    pallas_call x5, Pallas kernels: 340 us -> 311 us  [call(): pl.pallas_call(kernel, grid=grid, in_specs=in_specs, out_specs=out_specs,...]
    reshape x11 -> x3, local copies, waits for them, and re-layouts: 8.01 us -> 1.23 us  [the longest x2 1.22 us: local_step(): vec_grads.append(small_sum[start:stop].reshape(-1))]
    unnamed x14 -> x21, local copies, waits for them, and re-layouts: 10.9 us -> 16.9 us
where the time goes in v2:
time: 344 us; the launch traced here: 338 us
  Pallas kernels  311 us (90%)
  local copies, waits for them, and re-layouts  25.5 us (7%)
    pallas_call x5, Pallas kernels, call(): pl.pallas_call(kernel, grid=grid, in_specs=in_specs, out_specs=out_specs,...  311 us
    unnamed x21, local copies, waits for them, and re-layouts  16.9 us

profile of v2, /device:TPU:0, one launch (start us, length us, event | category | flops | bytes accessed | tf_op | source)
XLA Modules:
  0.0 338.1 jit_solution(697446905342304810)
XLA Ops:
  0.6 1.3 reshape.85.tok_seq
  1.9 0.9 dynamic-update-slice
  2.8 0.9 dynamic-update-slice.1
  3.7 0.9 dynamic-update-slice.2
  4.5 0.9 dynamic-update-slice.3
  5.4 0.9 dynamic-update-slice.4
  6.2 0.9 dynamic-update-slice.5
  7.1 0.9 dynamic-update-slice.6
  7.9 0.9 dynamic-update-slice.7
  8.8 0.8 fusion.1
  9.6 0.6 pad.9.vec_part
  10.2 16.3 %qkv.1 = (bf16[1536,768]{1,0:T(8,128)(2,1)}, bf16[1536,768]{1,0:T(8,128)(2,1)}, bf16[1536,768]{1,0:T(8,128)(2,1)}, bf16[1536,768]{1,0:T(8,128)(2,1)}, bf16[2,64,...) custom-call(s32[2,1,768]{2,1,0:T(1,128)} %reshape.85.tok_seq, ...), custom_call_target="tpu_custom_call" | custom-call | flops 5435817984 | bytes 31610880 | tf_op jit(solution)/shard_map/qkv/pallas_call | solution.py:334
  26.5 29.2 %attn_fwd.1 = (bf16[1536,768]{1,0:T(8,128)(2,1)}, f32[12,2,768]{2,1,0:T(2,128)}) custom-call(bf16[1536,768]{1,0:T(8,128)(2,1)} %get-tuple-element.43.q, bf16[1536,768]{1,0:T(8,128)(2,1)} %get-tuple-element.44.k, bf16[1536,768]{1,0:T(8,128)(2,1)} %get-tuple-element.45.v, s32[2,1,768]{2,1,0:T(1,128)} %reshape.85.tok_seq), custom_call_target="tpu_custom_call" | custom-call | flops 14495514624 | bytes 9517056 | tf_op jit(solution)/shard_map/attn_fwd/pallas_call | solution.py:334
  55.7 78.8 %ffn.1 = (bf16[1536,768]{1,0:T(8,128)(2,1)}, f32[1536,768]{1,0:T(8,128)}, bf16[1536,768]{1,0:T(8,128)(2,1)}, f32[768,768]{1,0:T(8,128)}, f32[4,768,768]{2,1,0:T(...) custom-call(bf16[1536,768]{1,0:T(8,128)(2,1)} %get-tuple-element.46.ctx, ...), custom_call_target="tpu_custom_call" | custom-call | flops 48922361856 | bytes 48500736 | tf_op jit(solution)/shard_map/ffn/pallas_call | solution.py:334
  134.5 72.4 %attn_bwd.1 = (bf16[1536,768]{1,0:T(8,128)(2,1)}, bf16[1536,768]{1,0:T(8,128)(2,1)}, bf16[1536,768]{1,0:T(8,128)(2,1)}, f32[12,3,128]{2,1,0:T(4,128)}, f32[3,2,8,768]{3,2,1,0:T(8,128)}) custom-call(bf16[1536,768]{1,0:T(8,128)(2,1)} %get-tuple-element.43.q, bf16[1536,768]{1,0:T(8,128)(2,1)} %get-tuple-element.44.k, bf16[1536,768]{1,0:T(8,128)(2,1)} %get-tuple-element.45.v, ...), custom_call_target="tpu_custom_call" | custom-call | flops 36238786560 | bytes 36421632 | tf_op jit(solution)/shard_map/attn_bwd/pallas_call | solution.py:334
  206.9 114.3 %qkv_bwd.1 = (f32[4,3,4,4,8,768]{5,4,3,2,1,0:T(8,128)}, f32[3,4,4,8,3072]{4,3,2,1,0:T(8,128)}, f32[3,4,4,8,768]{4,3,2,1,0:T(8,128)}, f32[3,4,4,8,2304]{4,3,2,1,0:T(8,128)}, f32[64,384]{1,0:T(8,128)}) custom-call(s32[2,1,768]{2,1,0:T(1,128)} %reshape.85.tok_seq, bf16[1536,768]{1,0:T(8,128)(2,1)} %get-tuple-element.47.x_in, ...), custom_call_target="tpu_custom_call" | custom-call | flops 10871635968 | bytes 34615296 | tf_op jit(solution)/shard_map/qkv_bwd/pallas_call | solution.py:334
  321.2 0.7 slice.30
  321.9 0.6 reshape.95
  322.6 0.7 slice.34
  323.3 0.6 reshape.101
  323.9 1.6 slice_reduce_fusion
  325.4 0.0 slice-start.2
  325.4 1.6 slice.27
  327.0 4.1 %copy.43 = f32[384,2304]{1,0:T(8,128)} copy(f32[384,2304]{1,0:T(8,128)} %bitcast.15) | data formatting | bytes 7077888
  331.2 0.0 copy-done
  331.2 1.0 copy.44
  332.2 0.0 slice-done.2
  332.2 0.0 slice-done.3
  332.2 2.4 copy.45
  334.6 0.8 slice-done
  335.4 0.3 slice-done.1
  335.8 2.2 copy.46
  (8 shorter events, 0.0 us)
Async XLA Ops:
  325.4 6.8 %slice-start.2 = ((s8[4718592]{0:T(1024)(128)(4,1)}), s8[4194304]{0:T(1024)(128)(4,1)S(1)}, s32[]{:S(2)}) async-start(s8[4718592]{0:T(1024)(128)(4,1)} %bitcast.12), calls=%async_computation.2 | async-start | bytes 8388608
  327.0 4.2 %copy-start = (f32[3,4,4,8,768]{4,3,2,1,0:T(8,128)S(1)}, f32[3,4,4,8,768]{4,3,2,1,0:T(8,128)}, u32[]{:S(2)}) copy-start(f32[3,4,4,8,768]{4,3,2,1,0:T(8,128)} %get-tuple-element.69) | copy-start | bytes 3538948
  327.0 5.2 %slice-start.3 = ((s8[4718592]{0:T(1024)(128)(4,1)}), s8[524288]{0:T(1024)(128)(4,1)S(1)}, s32[]{:S(2)}) async-start(s8[4718592]{0:T(1024)(128)(4,1)} %bitcast.12), calls=%async_computation.3 | async-start | bytes 1048576
  331.2 4.2 %slice-start = ((s8[4718592]{0:T(1024)(128)(4,1)}), s8[4194304]{0:T(1024)(128)(4,1)S(1)}, s32[]{:S(2)}) async-start(s8[4718592]{0:T(1024)(128)(4,1)} %bitcast.9), calls=%async_computation | async-start | bytes 8388608
  332.2 3.5 %slice-start.1 = ((s8[4718592]{0:T(1024)(128)(4,1)}), s8[524288]{0:T(1024)(128)(4,1)S(1)}, s32[]{:S(2)}) async-start(s8[4718592]{0:T(1024)(128)(4,1)} %bitcast.9), calls=%async_computation.1 | async-start | bytes 1048576

commit v3 on v2

--- a/solution.py
+++ b/solution.py
@@ -409,7 +409,7 @@
         scratch=[pltpu.VMEM((RING, 2) + blocks, F32)] * 2
         + comm_temps(2, blocks[3], dim) + sems(n_sems, n_sems, 2), name='attn_bwd', collective_id=0)
 
-    n_sems = 16 + 12 * FLOW_SEMS
+    n_sems = 16 + 18 * FLOW_SEMS
     fc2, fc1, out, qkv, small_sum = call(
         qkv_bwd_reduce_kernel, (seqs,),
         [pl.BlockSpec((1, 1, seq_len), lambda i: (i, 0, 0))] + [rows_spec(seq_len)] * 5
@@ -430,6 +430,7 @@
 
 RING = 4
 ALL = slice(None)
+DIRECT = 2
 ORDERS = ('xyz', 'yzx', 'zxy')
 STRIDE = {'x': 1, 'y': RING, 'z': RING * RING}
 MESH_ID = pl.DeviceIdType.MESH
@@ -452,7 +453,7 @@
 
     def greet(self):
         barrier = pltpu.get_barrier_semaphore()
-        peers = [self.partner()] + [self.chip(axis, delta) for axis in 'xyz' for delta in (1, -1)]
+        peers = [self.partner()] + [self.chip(axis, delta) for axis in 'xyz' for delta in (1, -1, 2)]
         for peer in peers:
             pl.semaphore_signal(barrier, inc=1, device_id=peer, device_id_type=MESH_ID)
         pl.semaphore_wait(barrier, len(peers))
@@ -471,16 +472,16 @@
         sign = self.sign
         if slot < 9:
             target = self.temp_view(self.temps, level, kind)
-            if kind == 2:
+            if kind == 2 and level != DIRECT:
                 return self.temp_view(self.temps, level, 0), target, level, sign
-            delta = (2, -sign)[kind]
-            return self.view(self.grads, self.place(level, delta)), target, level, (sign, -sign)[kind]
-        if kind == 2:
+            delta = (2, -sign, sign)[kind]
+            return self.view(self.grads, self.place(level, delta)), target, level, delta if level == DIRECT or kind else sign
+        if kind == 2 and level != DIRECT:
             block = self.view(self.sums, self.place(level, -sign))
             return block, block, level, sign
         target = self.view(self.sums, self.place(level + 1))
-        source = self.final(self) if level == 2 else target
-        return source, target, level, (sign, -sign)[kind]
+        source = self.final(self) if level == DIRECT else target
+        return source, target, level, (sign, -sign, 2)[kind]
 
     def copy(self, slot):
         src, dst, level, delta = self.route(slot)
@@ -500,39 +501,50 @@
         own = [self.torus.coord[axis] for axis in self.order[:level]]
         return tuple(own) + (() if delta is None else (self.torus.at(self.order[level], delta),))
 
+    def start_level(self, first, level):
+        for kind in range(3 if level == DIRECT else 2):
+            self.start(first + kind)
+
+    def wait_level(self, first, level):
+        for kind in range(0 if level == DIRECT else 1, 3):
+            self.wait(first + kind)
+
     def scatter_start(self, level):
-        self.start(level * 3)
-        self.start(level * 3 + 1)
+        self.start_level(level * 3, level)
 
     def scatter_mid(self, level):
+        if level == DIRECT:
+            return
         self.wait(level * 3)
         relay = self.temp_view(self.temps, level, 0)
         relay[...] = relay[...] + self.view(self.grads, self.place(level, self.sign))[...]
         self.start(level * 3 + 2)
 
     def scatter_end(self, level):
-        self.wait(level * 3 + 1)
-        self.wait(level * 3 + 2)
+        self.wait_level(level * 3, level)
         mine = self.view(self.grads, self.place(level, 0))
-        mine[...] = mine[...] + self.temp_view(self.temps, level, 1)[...] + self.temp_view(self.temps, level, 2)[...]
+        total = mine[...]
+        for kind in range(0 if level == DIRECT else 1, 3):
+            total = total + self.temp_view(self.temps, level, kind)[...]
+        mine[...] = total
 
     def gather_start(self, level):
-        if level == 2:
+        if level == DIRECT:
             self.view(self.sums, self.place(3))[...] = self.final(self)[...]
-        self.start(9 + level * 3)
-        self.start(10 + level * 3)
+        self.start_level(9 + level * 3, level)
 
     def gather_mid(self, level):
+        if level == DIRECT:
+            return
         self.wait(9 + level * 3)
         self.start(11 + level * 3)
 
     def gather_end(self, level):
-        self.wait(10 + level * 3)
-        self.wait(11 + level * 3)
+        self.wait_level(9 + level * 3, level)
 
     def scatter_next(self, level):
         self.scatter_end(level)
-        if level == 2:
+        if level == DIRECT:
             self.gather_start(level)
         else:
             self.scatter_start(level + 1)
@@ -555,12 +567,13 @@
 
 
 def make_flows(torus, width, grads, sums, temps, sends, recvs, base, group=ALL, temp_group=ALL, final=own_block,
-               spacing=FLOW_SEMS):
+               spacing=FLOW_SEMS, pieces=None):
     half = width // 2
     flows = []
-    for color, order in enumerate(ORDERS):
-        for side, sign in enumerate((1, -1)):
-            lanes = pl.ds(side * half, half)
+    for first, size in pieces or ((0, half),):
+        for color, order, side in [(color, order, side) for color, order in enumerate(ORDERS) for side in range(2)]:
+            sign = 1 - 2 * side
+            lanes = pl.ds(side * half + first, size)
 
             def view(ref, place, color=color, lanes=lanes):
                 rest = place[1:] + (ALL,) * (4 - len(place))
@@ -585,7 +598,7 @@
     return [pltpu.VMEM((3, groups, 3) + (RING,) * (2 - level) + (rows, dim), F32) for level in range(3)]
 
 
-PLAN = ('b', '', 'e0', '', '', 'm00 e1', '', 'a00', 'm01 m10', 'a01', 'm02 a10', 'm11 a02', 'a11 m12 a12')
+PLAN = ('b', '', 'e0', '', 'e1', 'm00', '', 'm10', 'a00', 'm01 a10', 'a01 m11', 'a11', 'a02 a12')
 
 
 def attn_bwd_reduce_kernel(q, k, v, d_ctx, lse, tok_seq, cos, sin, fc2, fc1, dq_out, dk_out, dv_out, sums_out, red,
@@ -663,7 +676,7 @@
 
     gathers = make_flows(torus, dim, None, sums_ab, None, sends, recvs, 16, final=final)
     flows = make_flows(torus, dim, grads, sums, (temp0, temp1, temp2), sends, recvs, 16 + 6 * FLOW_SEMS,
-                       group=pl.ds(part, 1))
+                       group=pl.ds(part, 1), pieces=((0, 2 * PAIR), (2 * PAIR, PAIR)))
 
     def load_out():
         return pltpu.make_async_copy(gw_out, grads.at[0], local.at[0])
@@ -812,9 +825,11 @@
          ln2_gain, ln2_bias, w_fc1, b_fc1, w_fc2, b_fc2) = shards
         vectors = (ln1_gain, ln1_bias, b_out, ln2_gain, ln2_bias, b_fc2, b_qkv, b_fc1)
         vocab, width = embedding.shape
-        flat = jnp.concatenate(vectors)
-        vec_part = jnp.concatenate([jnp.pad(embedding, ((0, VEC_ROW - vocab), (0, 0))), flat.reshape(-1, width)])
-        vec_part = jnp.pad(vec_part, ((0, SMALL_ROWS - vec_part.shape[0]), (0, 0)))
+        rows = [vec[first:first + width] for vec in vectors for first in range(0, vec.size, width)]
+        at_row = jnp.asarray(np.indices((SMALL_ROWS, width))[0], jnp.int32)
+        vec_part = jnp.pad(embedding, ((0, SMALL_ROWS - vocab), (0, 0)))
+        for index, row in enumerate(rows):
+            vec_part = jnp.where(at_row == VEC_ROW + index, row[None, :], vec_part)
         hidden, big, small_sum = layer_compute(tokens, grad_y, vec_part, (w_qkv, w_out, w_fc1, w_fc2))
         g_w_qkv, g_w_out, g_w_fc1, g_w_fc2 = big
         g_embedding = small_sum[:vocab]

time: 344 us -> 318 us (0.924); the launches traced: 338 us -> 320 us
  Pallas kernels: 311 us -> 299 us
  local copies, waits for them, and re-layouts: 25.5 us -> 18.8 us
    pallas_call x5, Pallas kernels: 311 us -> 299 us  [call(): pl.pallas_call(kernel, grid=grid, in_specs=in_specs, out_specs=out_specs,...]
    unnamed x21 -> x14, local copies, waits for them, and re-layouts: 16.9 us -> 10.9 us
where the time goes in v3:
time: 318 us; the launch traced here: 320 us
  Pallas kernels  299 us (94%)
  local copies, waits for them, and re-layouts  18.8 us (6%)
    pallas_call x5, Pallas kernels, call(): pl.pallas_call(kernel, grid=grid, in_specs=in_specs, out_specs=out_specs,...  299 us
    unnamed x14, local copies, waits for them, and re-layouts  10.9 us

profile of v3, /device:TPU:0, one launch (start us, length us, event | category | flops | bytes accessed | tf_op | source)
XLA Modules:
  0.0 320.2 jit_solution(12595364105847341819)
XLA Ops:
  0.6 1.3 reshape.95.tok_seq
  1.9 0.8 fusion
  2.7 1.7 select_select_fusion.vec_part
  4.5 16.3 %qkv.1 = (bf16[1536,768]{1,0:T(8,128)(2,1)}, bf16[1536,768]{1,0:T(8,128)(2,1)}, bf16[1536,768]{1,0:T(8,128)(2,1)}, bf16[1536,768]{1,0:T(8,128)(2,1)}, bf16[2,64,...) custom-call(s32[2,1,768]{2,1,0:T(1,128)} %reshape.95.tok_seq, ...), custom_call_target="tpu_custom_call" | custom-call | flops 5435817984 | bytes 31610880 | tf_op jit(solution)/shard_map/qkv/pallas_call | solution.py:334
  20.8 29.2 %attn_fwd.1 = (bf16[1536,768]{1,0:T(8,128)(2,1)}, f32[12,2,768]{2,1,0:T(2,128)}) custom-call(bf16[1536,768]{1,0:T(8,128)(2,1)} %get-tuple-element.43.q, bf16[1536,768]{1,0:T(8,128)(2,1)} %get-tuple-element.44.k, bf16[1536,768]{1,0:T(8,128)(2,1)} %get-tuple-element.45.v, s32[2,1,768]{2,1,0:T(1,128)} %reshape.95.tok_seq), custom_call_target="tpu_custom_call" | custom-call | flops 14495514624 | bytes 9517056 | tf_op jit(solution)/shard_map/attn_fwd/pallas_call | solution.py:334
  49.9 80.2 %ffn.1 = (bf16[1536,768]{1,0:T(8,128)(2,1)}, f32[1536,768]{1,0:T(8,128)}, bf16[1536,768]{1,0:T(8,128)(2,1)}, f32[768,768]{1,0:T(8,128)}, f32[4,768,768]{2,1,0:T(...) custom-call(bf16[1536,768]{1,0:T(8,128)(2,1)} %get-tuple-element.46.ctx, ...), custom_call_target="tpu_custom_call" | custom-call | flops 48922361856 | bytes 48500736 | tf_op jit(solution)/shard_map/ffn/pallas_call | solution.py:334
  130.1 62.6 %attn_bwd.1 = (bf16[1536,768]{1,0:T(8,128)(2,1)}, bf16[1536,768]{1,0:T(8,128)(2,1)}, bf16[1536,768]{1,0:T(8,128)(2,1)}, f32[12,3,128]{2,1,0:T(4,128)}, f32[3,2,8,768]{3,2,1,0:T(8,128)}) custom-call(bf16[1536,768]{1,0:T(8,128)(2,1)} %get-tuple-element.43.q, bf16[1536,768]{1,0:T(8,128)(2,1)} %get-tuple-element.44.k, bf16[1536,768]{1,0:T(8,128)(2,1)} %get-tuple-element.45.v, ...), custom_call_target="tpu_custom_call" | custom-call | flops 36238786560 | bytes 36421632 | tf_op jit(solution)/shard_map/attn_bwd/pallas_call | solution.py:334
  192.7 110.5 %qkv_bwd.1 = (f32[4,3,4,4,8,768]{5,4,3,2,1,0:T(8,128)}, f32[3,4,4,8,3072]{4,3,2,1,0:T(8,128)}, f32[3,4,4,8,768]{4,3,2,1,0:T(8,128)}, f32[3,4,4,8,2304]{4,3,2,1,0:T(8,128)}, f32[64,384]{1,0:T(8,128)}) custom-call(s32[2,1,768]{2,1,0:T(1,128)} %reshape.95.tok_seq, bf16[1536,768]{1,0:T(8,128)(2,1)} %get-tuple-element.47.x_in, ...), custom_call_target="tpu_custom_call" | custom-call | flops 10871635968 | bytes 34615296 | tf_op jit(solution)/shard_map/qkv_bwd/pallas_call | solution.py:334
  303.2 0.7 slice.58
  303.9 0.6 reshape.104
  304.5 0.7 slice.62
  305.2 0.6 reshape.110
  305.9 1.6 slice_reduce_fusion
  307.4 0.0 slice-start.2
  307.4 1.6 slice.55
  309.0 0.0 copy-start
  309.0 0.0 slice-start.3
  309.0 4.1 %copy.49 = f32[384,2304]{1,0:T(8,128)} copy(f32[384,2304]{1,0:T(8,128)} %bitcast.15) | data formatting | bytes 7077888
  313.2 0.0 copy-done
  313.2 0.0 slice-start
  313.2 1.0 copy.50
  314.2 0.0 slice-done.2
  314.2 0.0 slice-done.3
  314.2 0.0 slice-start.1
  314.2 2.4 copy.51
  316.6 0.8 slice-done
  317.4 0.3 slice-done.1
  317.7 2.2 copy.52
  (2 shorter events, 0.0 us)
Async XLA Ops:
  307.4 6.8 %slice-start.2 = ((s8[4718592]{0:T(1024)(128)(4,1)}), s8[4194304]{0:T(1024)(128)(4,1)S(1)}, s32[]{:S(2)}) async-start(s8[4718592]{0:T(1024)(128)(4,1)} %bitcast.12), calls=%async_computation.2 | async-start | bytes 8388608
  309.0 4.2 %copy-start = (f32[3,4,4,8,768]{4,3,2,1,0:T(8,128)S(1)}, f32[3,4,4,8,768]{4,3,2,1,0:T(8,128)}, u32[]{:S(2)}) copy-start(f32[3,4,4,8,768]{4,3,2,1,0:T(8,128)} %get-tuple-element.69) | copy-start | bytes 3538948
  309.0 5.2 %slice-start.3 = ((s8[4718592]{0:T(1024)(128)(4,1)}), s8[524288]{0:T(1024)(128)(4,1)S(1)}, s32[]{:S(2)}) async-start(s8[4718592]{0:T(1024)(128)(4,1)} %bitcast.12), calls=%async_computation.3 | async-start | bytes 1048576
  313.2 4.2 %slice-start = ((s8[4718592]{0:T(1024)(128)(4,1)}), s8[4194304]{0:T(1024)(128)(4,1)S(1)}, s32[]{:S(2)}) async-start(s8[4718592]{0:T(1024)(128)(4,1)} %bitcast.9), calls=%async_computation | async-start | bytes 8388608
  314.2 3.5 %slice-start.1 = ((s8[4718592]{0:T(1024)(128)(4,1)}), s8[524288]{0:T(1024)(128)(4,1)S(1)}, s32[]{:S(2)}) async-start(s8[4718592]{0:T(1024)(128)(4,1)} %bitcast.9), calls=%async_computation.1 | async-start | bytes 1048576

commit v4 on v3

--- a/solution.py
+++ b/solution.py
@@ -360,7 +360,7 @@
     def sems(*counts):
         return [pltpu.SemaphoreType.DMA((n,)) for n in counts]
 
-    tile = 256
+    tile = 384
     per_seq = seq_len // tile
     table_spec = pl.BlockSpec((tile, PAIR), lambda i: (i % per_seq, 0))
     full = [shape_of((2 * w.shape[0],) + w.shape[1:], BF16) for w in weights]
@@ -681,15 +681,12 @@
     def load_out():
         return pltpu.make_async_copy(gw_out, grads.at[0], local.at[0])
 
-    def later_hook():
-        each(gathers, 'gather_next', 2)
+    def middle_hook():
         each(gathers, 'gather_mid', 1)
-
-    def last_hook():
-        each(gathers, 'gather_next', 1)
         load_out().wait()
 
-    hooks = ((0, 1, lambda: each(gathers, 'gather_mid', 2)), (0, 2, later_hook), (1, 0, last_hook))
+    hooks = ((0, 1, lambda: each(gathers, 'gather_next', 2)), (1, 0, middle_hook),
+             (1, 1, lambda: each(gathers, 'gather_next', 1)))
 
     def pair_copy(page):
         return pltpu.make_async_remote_copy(

time: 318 us -> 317 us (level)
  no operation moved by 1% of the time
where the time goes in v4:
time: 317 us; the launch traced here: 318 us
  Pallas kernels  297 us (94%)
  local copies, waits for them, and re-layouts  18.8 us (6%)
    pallas_call x5, Pallas kernels, call(): pl.pallas_call(kernel, grid=grid, in_specs=in_specs, out_specs=out_specs,...  297 us
    unnamed x14, local copies, waits for them, and re-layouts  10.9 us

profile of v4, /device:TPU:0, one launch (start us, length us, event | category | flops | bytes accessed | tf_op | source)
XLA Modules:
  0.0 318.4 jit_solution(937773755231583993)
XLA Ops:
  0.6 1.3 reshape.95.tok_seq
  1.9 0.8 fusion
  2.7 1.7 select_select_fusion.vec_part
  4.5 15.7 %qkv.1 = (bf16[1536,768]{1,0:T(8,128)(2,1)}, bf16[1536,768]{1,0:T(8,128)(2,1)}, bf16[1536,768]{1,0:T(8,128)(2,1)}, bf16[1536,768]{1,0:T(8,128)(2,1)}, bf16[2,64,...) custom-call(s32[2,1,768]{2,1,0:T(1,128)} %reshape.95.tok_seq, ...), custom_call_target="tpu_custom_call" | custom-call | flops 5435817984 | bytes 31610880 | tf_op jit(solution)/shard_map/qkv/pallas_call | solution.py:334
  20.2 29.2 %attn_fwd.1 = (bf16[1536,768]{1,0:T(8,128)(2,1)}, f32[12,2,768]{2,1,0:T(2,128)}) custom-call(bf16[1536,768]{1,0:T(8,128)(2,1)} %get-tuple-element.43.q, bf16[1536,768]{1,0:T(8,128)(2,1)} %get-tuple-element.44.k, bf16[1536,768]{1,0:T(8,128)(2,1)} %get-tuple-element.45.v, s32[2,1,768]{2,1,0:T(1,128)} %reshape.95.tok_seq), custom_call_target="tpu_custom_call" | custom-call | flops 14495514624 | bytes 9517056 | tf_op jit(solution)/shard_map/attn_fwd/pallas_call | solution.py:334
  49.4 80.2 %ffn.1 = (bf16[1536,768]{1,0:T(8,128)(2,1)}, f32[1536,768]{1,0:T(8,128)}, bf16[1536,768]{1,0:T(8,128)(2,1)}, f32[768,768]{1,0:T(8,128)}, f32[4,768,768]{2,1,0:T(...) custom-call(bf16[1536,768]{1,0:T(8,128)(2,1)} %get-tuple-element.46.ctx, ...), custom_call_target="tpu_custom_call" | custom-call | flops 48922361856 | bytes 48500736 | tf_op jit(solution)/shard_map/ffn/pallas_call | solution.py:334
  129.5 62.6 %attn_bwd.1 = (bf16[1536,768]{1,0:T(8,128)(2,1)}, bf16[1536,768]{1,0:T(8,128)(2,1)}, bf16[1536,768]{1,0:T(8,128)(2,1)}, f32[12,3,128]{2,1,0:T(4,128)}, f32[3,2,8,768]{3,2,1,0:T(8,128)}) custom-call(bf16[1536,768]{1,0:T(8,128)(2,1)} %get-tuple-element.43.q, bf16[1536,768]{1,0:T(8,128)(2,1)} %get-tuple-element.44.k, bf16[1536,768]{1,0:T(8,128)(2,1)} %get-tuple-element.45.v, ...), custom_call_target="tpu_custom_call" | custom-call | flops 36238786560 | bytes 36421632 | tf_op jit(solution)/shard_map/attn_bwd/pallas_call | solution.py:334
  192.1 109.3 %qkv_bwd.1 = (f32[4,3,4,4,8,768]{5,4,3,2,1,0:T(8,128)}, f32[3,4,4,8,3072]{4,3,2,1,0:T(8,128)}, f32[3,4,4,8,768]{4,3,2,1,0:T(8,128)}, f32[3,4,4,8,2304]{4,3,2,1,0:T(8,128)}, f32[64,384]{1,0:T(8,128)}) custom-call(s32[2,1,768]{2,1,0:T(1,128)} %reshape.95.tok_seq, bf16[1536,768]{1,0:T(8,128)(2,1)} %get-tuple-element.47.x_in, ...), custom_call_target="tpu_custom_call" | custom-call | flops 10871635968 | bytes 34615296 | tf_op jit(solution)/shard_map/qkv_bwd/pallas_call | solution.py:334
  301.4 0.7 slice.58
  302.1 0.6 reshape.104
  302.8 0.7 slice.62
  303.5 0.6 reshape.110
  304.1 1.6 slice_reduce_fusion
  305.6 0.0 slice-start.2
  305.6 1.6 slice.55
  307.2 0.0 copy-start
  307.2 0.0 slice-start.3
  307.2 4.1 %copy.49 = f32[384,2304]{1,0:T(8,128)} copy(f32[384,2304]{1,0:T(8,128)} %bitcast.15) | data formatting | bytes 7077888
  311.4 0.0 copy-done
  311.4 0.0 slice-start
  311.4 1.0 copy.50
  312.4 0.0 slice-done.2
  312.4 0.0 slice-done.3
  312.4 0.0 slice-start.1
  312.4 2.4 copy.51
  314.8 0.8 slice-done
  315.6 0.3 slice-done.1
  316.0 2.2 copy.52
  (2 shorter events, 0.0 us)
Async XLA Ops:
  305.6 6.8 %slice-start.2 = ((s8[4718592]{0:T(1024)(128)(4,1)}), s8[4194304]{0:T(1024)(128)(4,1)S(1)}, s32[]{:S(2)}) async-start(s8[4718592]{0:T(1024)(128)(4,1)} %bitcast.12), calls=%async_computation.2 | async-start | bytes 8388608
  307.2 4.2 %copy-start = (f32[3,4,4,8,768]{4,3,2,1,0:T(8,128)S(1)}, f32[3,4,4,8,768]{4,3,2,1,0:T(8,128)}, u32[]{:S(2)}) copy-start(f32[3,4,4,8,768]{4,3,2,1,0:T(8,128)} %get-tuple-element.69) | copy-start | bytes 3538948
  307.2 5.2 %slice-start.3 = ((s8[4718592]{0:T(1024)(128)(4,1)}), s8[524288]{0:T(1024)(128)(4,1)S(1)}, s32[]{:S(2)}) async-start(s8[4718592]{0:T(1024)(128)(4,1)} %bitcast.12), calls=%async_computation.3 | async-start | bytes 1048576
  311.4 4.2 %slice-start = ((s8[4718592]{0:T(1024)(128)(4,1)}), s8[4194304]{0:T(1024)(128)(4,1)S(1)}, s32[]{:S(2)}) async-start(s8[4718592]{0:T(1024)(128)(4,1)} %bitcast.9), calls=%async_computation | async-start | bytes 8388608
  312.4 3.5 %slice-start.1 = ((s8[4718592]{0:T(1024)(128)(4,1)}), s8[524288]{0:T(1024)(128)(4,1)S(1)}, s32[]{:S(2)}) async-start(s8[4718592]{0:T(1024)(128)(4,1)} %bitcast.9), calls=%async_computation.1 | async-start | bytes 1048576
